TPU v7x, 32 devices: a whole 2x2x4 slice. The times are simulated.
32 devices in a mesh: pool: 2 (over x), seq: 4 (over y, core), head: 4 (over z).
Axes of the slice: x: 2, y: 2, z: 4, core: 2. Of those that a mesh axis runs over, the one named last changes fastest.
Arguments:
- prompt: bfloat16 [8, 2048, 8192], P('pool', 'seq'), may hold values from -6 to 6
- key_value_weight: bfloat16 [8192, 2, 1024], P('seq', None, 'head'), may hold values from -0.0625 to 0.0625
- adapter_down_weight: bfloat16 [8192, 256], P('seq'), may hold values from -0.0625 to 0.0625
- adapter_up_weight: bfloat16 [8, 2, 16, 1024], P(None, None, None, 'head'), may hold values from -0.75 to 0.75
- request_adapter_index: int32 [8], P('pool'), may hold values from 0 to 7
- destination: int32 [8], replicated, may hold values from 0 to 3, as said below
- rotated_query: bfloat16 [384, 8192], P(('pool', 'seq'), 'head'), may hold values from -150 to 150
- key_value_cache: bfloat16 [384, 128, 2, 1024], P(('pool', 'seq'), None, None, 'head'), may hold values from -6 to 6
- current_key_value: bfloat16 [384, 2, 1024], P(('pool', 'seq'), None, 'head'), may hold values from -6 to 6
- cached_length: int32 [384], P(('pool', 'seq')), may hold values from 1 to 128
- row_adapter_index: int32 [384], P('pool'), may hold values from 0 to 7
- output_weight: bfloat16 [8192, 8192], P('head', 'seq'), may hold values from -0.0625 to 0.0625
- output_down_weight: bfloat16 [8192, 8, 16], P('head'), may hold values from -0.0625 to 0.0625
- output_up_weight: bfloat16 [8, 16, 8192], P(None, None, 'seq'), may hold values from -3.59375 to 3.59375
Outputs:
- handed: bfloat16 [8, 2, 2048, 2, 1024], P(('pool', 'seq'), None, None, None, 'head')
- decoded: bfloat16 [384, 8192], P(('pool', 'head'), 'seq')
Inputs may be any that keep to these rules, and one draw needn't show every extreme that they name: `destination`: among one pool's 4 requests no decode owner is named more than 2 times, and some owner exactly 2 times; in each pool owners 0 and 3 both receive requests.
All inputs are finite; a program needn't handle non-finite values.
Results may differ from a plain program's by a relative error of at most 0.0085.
Values may be sent and summed in bfloat16 or wider, within the bound.
A program may use at most 128 MiB of HBM per device.

v0:
```python
import jax
import jax.numpy as jnp
from jax import lax
from jax.sharding import PartitionSpec as P

HEAD_DIM = 128
ADAPTER_RANK = 16
ADAPTER_COUNT = 8
CAP = 2


def swapped(value, axis, distance):
    mask = 2**distance
    pairs = [(source, source ^ mask) for source in range(lax.axis_size(axis))]
    return lax.ppermute(value, axis, pairs)


def attend_local(query_matrix, key_value_cache, prefill_state, lengths):
    decode_count = query_matrix.shape[0]
    kv_heads = key_value_cache.shape[-1] // HEAD_DIM
    query_groups = query_matrix.shape[1] // HEAD_DIM // kv_heads
    positions = key_value_cache.shape[1]
    query_batch = query_matrix.reshape(decode_count, kv_heads, query_groups, HEAD_DIM)
    key_matrix = key_value_cache[:, :, 0].reshape(decode_count, positions, kv_heads, HEAD_DIM)
    value_matrix = key_value_cache[:, :, 1].reshape(decode_count, positions, kv_heads, HEAD_DIM)
    prefill_key = prefill_state[:, 0].reshape(decode_count, kv_heads, HEAD_DIM)
    prefill_value = prefill_state[:, 1].reshape(decode_count, kv_heads, HEAD_DIM)
    factor = HEAD_DIM ** (-0.5)
    scores = (
        jnp.einsum("rkgd,rckd->rkgc", query_batch, key_matrix, preferred_element_type=jnp.float32)
        * factor
    )
    own_score = (
        jnp.einsum("rkgd,rkd->rkg", query_batch, prefill_key, preferred_element_type=jnp.float32)
        * factor
    )
    valid = (jnp.arange(positions, dtype=jnp.int32)[None, :] < lengths[:, None])[:, None, None, :]
    highest = jnp.maximum(jnp.max(jnp.where(valid, scores, -1e30), axis=-1), own_score)
    raw = jnp.where(valid, jnp.exp(scores - highest[..., None]), 0.0)
    own_raw = jnp.exp(own_score - highest)
    normer = jnp.sum(raw, axis=-1) + own_raw
    weights = (raw / normer[..., None]).astype(jnp.bfloat16)
    own_weight = (own_raw / normer).astype(jnp.bfloat16)
    mixed = jnp.einsum("rkgc,rckd->rkgd", weights, value_matrix, preferred_element_type=jnp.float32)
    mixed = (
        mixed
        + own_weight.astype(jnp.float32)[..., None]
        * prefill_value.astype(jnp.float32)[:, :, None, :]
    )
    return mixed.reshape(decode_count, kv_heads * query_groups * HEAD_DIM).astype(jnp.bfloat16)


def place_slots(owner_ids, block, decoders):
    requests = block.shape[0]
    order_index = jnp.arange(requests, dtype=jnp.int32)
    same_owner = owner_ids[:, None] == owner_ids[None, :]
    slot_of = jnp.sum(
        (same_owner & (order_index[None, :] < order_index[:, None])).astype(jnp.int32), axis=1
    )
    slot_hit = slot_of[None, :] == jnp.arange(CAP, dtype=jnp.int32)[:, None]
    owner_hit = owner_ids[None, :] == jnp.arange(decoders, dtype=jnp.int32)[:, None]
    placer = (slot_hit[:, None, :] & owner_hit[None, :, :]).astype(jnp.bfloat16)
    flat = block.reshape(requests, block.shape[1] * block.shape[2] * block.shape[3])
    outgoing = jnp.einsum("cdr,rx->cdx", placer, flat, preferred_element_type=jnp.float32)
    return outgoing.astype(jnp.bfloat16).reshape(
        CAP, decoders, block.shape[1], block.shape[2], block.shape[3]
    )


def body(
    prompt,
    key_value_weight,
    adapter_down_weight,
    adapter_up_weight,
    request_adapter_index,
    destination,
    rotated_query,
    key_value_cache,
    current_key_value,
    cached_length,
    row_adapter_index,
    output_weight,
    output_down_weight,
    output_up_weight,
):
    requests, tok_dev, model_width = prompt.shape
    key_value_width = key_value_weight.shape[2]
    token_matrix = prompt.reshape(requests * tok_dev, model_width)
    weight_rows = lax.all_gather(key_value_weight, "seq", axis=0, tiled=True)
    lowered_rows = lax.all_gather(adapter_down_weight, "seq", axis=0, tiled=True)
    decode_count = weight_rows.shape[0]
    base_part = jnp.dot(
        token_matrix,
        weight_rows.reshape(decode_count, 2 * key_value_width),
        preferred_element_type=jnp.float32,
    )
    low_part = jnp.dot(token_matrix, lowered_rows, preferred_element_type=jnp.float32)
    reduced_everything = low_part
    adapter_selector = (
        request_adapter_index[:, None] == jnp.arange(ADAPTER_COUNT, dtype=jnp.int32)[None, :]
    )
    reduced_everything = reduced_everything.reshape(
        requests, tok_dev, ADAPTER_COUNT, 2, ADAPTER_RANK
    )
    low_rank = jnp.sum(
        jnp.where(adapter_selector[:, None, :, None, None], reduced_everything, 0.0), axis=2
    )
    selected_up_weight = jnp.einsum(
        "um,mdzt->udzt",
        adapter_selector.astype(jnp.bfloat16),
        adapter_up_weight,
        preferred_element_type=jnp.float32,
    )
    correction = jnp.einsum(
        "rtkq,rkqf->rtkf", low_rank, selected_up_weight, precision=lax.Precision.HIGHEST
    )
    prefilled = (base_part.reshape(requests, tok_dev, 2, key_value_width) + correction).astype(
        jnp.bfloat16
    )
    decoders = lax.axis_size("seq")
    pool_index = lax.axis_index("pool")
    other_owners = lax.dynamic_slice_in_dim(destination, (1 - pool_index) * requests, requests)
    arrived = swapped(prefilled, "pool", 0)
    outgoing = place_slots(other_owners, arrived, decoders)
    handed = lax.all_to_all(outgoing, "seq", split_axis=1, concat_axis=1, tiled=True)
    handed = handed.reshape(1, CAP, decoders * tok_dev, 2, key_value_width)
    attended = attend_local(rotated_query, key_value_cache, current_key_value, cached_length)
    down_flat = output_down_weight.reshape(
        output_down_weight.shape[0], ADAPTER_COUNT * ADAPTER_RANK
    )
    up_flat = output_up_weight.reshape(
        ADAPTER_COUNT * ADAPTER_RANK, output_up_weight.shape[2]
    ).astype(jnp.float32)
    rank_owner = jnp.arange(ADAPTER_COUNT * ADAPTER_RANK, dtype=jnp.int32) // ADAPTER_RANK
    attn_rows = lax.all_gather(attended, "seq", axis=0, tiled=True)
    low_rows = jnp.dot(attn_rows, down_flat, preferred_element_type=jnp.float32)
    low_rows = jnp.where(row_adapter_index[:, None] == rank_owner[None, :], low_rows, 0.0)
    projected = jnp.dot(attn_rows, output_weight, preferred_element_type=jnp.float32)
    terms = projected + jnp.dot(low_rows, up_flat, precision=lax.Precision.HIGHEST)
    decoded = lax.psum_scatter(terms, "head", scatter_dimension=0, tiled=True)
    return (handed, decoded.astype(jnp.bfloat16))


def solution(mesh):
    in_specs = (
        P("pool", "seq", None),
        P("seq", None, "head"),
        P("seq", None),
        P(None, None, None, "head"),
        P("pool"),
        P(),
        P(("pool", "seq"), "head"),
        P(("pool", "seq"), None, None, "head"),
        P(("pool", "seq"), None, "head"),
        P(("pool", "seq")),
        P("pool"),
        P("head", "seq"),
        P("head", None, None),
        P(None, None, "seq"),
    )
    out_specs = (P(("pool", "seq"), None, None, None, "head"), P(("pool", "head"), "seq"))
    return jax.shard_map(body, mesh=mesh, in_specs=in_specs, out_specs=out_specs, check_vma=False)
```

profile of v0, /device:TPU:0, one launch (start us, length us, event | category | flops | bytes accessed | tf_op | source)
XLA Modules:
  0.0 321.1 jit_solution(5121571751977776219)
XLA Ops:
  8.1 2.4 copy.68
  10.5 0.7 all-gather.3.cloned.1.call-update
  11.2 13.9 %fusion.29 = (bf16[48,128,1,256]{3,2,1,0:T(2,128)(2,1)}, bf16[48,128,1,256]{3,2,1,0:T(2,128)(2,1)}) fusion(bf16[48,128,2,256]{3,2,1,0:T(2,128)(2,1)} %param.21), kind=kLoop, calls=%fused_computation.52 | loop fusion | bytes 12582912 | tf_op jit(solution)/shard_map/slice | solution.py:24
  25.2 13.5 %copy.93 = bf16[48,128,1,256]{1,3,0,2:T(8,128)(2,1)} copy(bf16[48,128,1,256]{3,2,1,0:T(2,128)(2,1)} %get-tuple-element.8) | data formatting | bytes 6291456
  38.8 2.9 select_reduce_fusion.1
  41.8 0.2 fusion.17
  42.3 0.4 fusion.9
  42.9 13.6 %copy.94 = bf16[48,128,1,256]{1,3,0,2:T(8,128)(2,1)} copy(bf16[48,128,1,256]{3,2,1,0:T(2,128)(2,1)} %get-tuple-element.9) | data formatting | bytes 6291456
  56.7 0.2 fusion.15
  56.9 4.2 %fusion.8 = bf16[48,2,8,128]{3,2,1,0:T(8,128)(2,1)S(1)} fusion(bf16[48,128,2,128]{1,3,2,0:T(8,128)(2,1)} %bitcast.84, f32[48,2,8,128]{3,2,1,0:T(8,128)S(1)} %get-tuple-element.13, f32[48,2,128]{2,1,0:T(2,128)S(1)} %bitcast.91, f32[48,2,8]{2,1,0:T(2,128)S(1)} %copy.82, f32[48,2,8]{2,1,0:T(2,128)S(1)} %copy.79, f32[48,2,8]{2,1,0:T(2,128)S(1)} %copy.77, ...), kind=kOutput, calls=%fused_computation.12 | convolution fusion | flops 25853952 | bytes 3800064 | tf_op jit(solution)/shard_map/rkgc,rckd->rkgd/dot_general | solution.py:44
  61.1 16.6 %select_reduce_fusion = f32[4,512,2,16]{1,3,2,0:T(8,128)S(1)} fusion(bf16[8,2,16,8192,1]{3,2,1,0,4:T(8,128)(2,1)} %bitcast.92, bf16[4,512,8192]{2,1,0:T(8,128)(2,1)} %param.14, pred[4,8]{1,0:T(4,128)(4,1)S(1)} %iota_compare_fusion.1), kind=kOutput, calls=%fused_computation.9 | convolution fusion | flops 8590917632 | bytes 38010912 | tf_op jit(solution)/shard_map/dot_general | solution.py:97
  77.7 29.9 %all-gather.3.cloned.1.call-done = bf16[8192,2,256]{2,1,0:T(2,128)(2,1)} async-done(((bf16[2048,2,256]{2,1,0:T(2,128)(2,1)}), bf16[8192,2,256]{2,1,0:T(2,128)(2,1)}) %all-gather.3.cloned.1.call-update) | async-done | bytes 8388624 | tf_op jit(solution)/shard_map/all_gather | solution.py:89
  107.6 21.2 %copy.92 = bf16[8192,2,256]{0,2,1:T(8,128)(2,1)} copy(bf16[8192,2,256]{2,1,0:T(2,128)(2,1)} %all-gather.3.cloned.1.call-done) | data formatting | bytes 16777216 | tf_op jit(solution)/shard_map/reshape | solution.py:94
  128.8 23.9 %fusion.2 = f32[4,512,2,256]{3,1,2,0:T(8,128)S(1)} fusion(bf16[4,512,8192]{2,1,0:T(8,128)(2,1)} %param.14, bf16[8192,2,256]{0,2,1:T(8,128)(2,1)} %copy.92), kind=kOutput, calls=%fused_computation.3 | convolution fusion | flops 17179869184 | bytes 46137344 | tf_op jit(solution)/shard_map/dot_general | solution.py:92
  152.7 4.0 %fusion.5 = bf16[4,512,2,256]{3,1,2,0:T(8,128)(2,1)S(1)} fusion(f32[4,512,2,256]{3,1,2,0:T(8,128)S(1)} %fusion.2, f32[4,512,2,16]{1,3,2,0:T(8,128)S(1)} %select_reduce_fusion, f32[4,2,16,256]{3,0,2,1:T(4,128)S(1)} %fusion.15), kind=kOutput, calls=%fused_computation.7 | convolution fusion | flops 203423744 | bytes 6684672 | tf_op jit(solution)/shard_map/rtkq,rkqf->rtkf/dot_general | solution.py:114
  156.7 1.5 collective-permute-start
  158.3 8.6 %all_gather.11 = bf16[192,2048]{1,0:T(8,128)(2,1)S(1)} all-gather(bf16[48,2048]{1,0:T(8,128)(2,1)S(1)} %bitcast.87), channel_id=1, replica_groups=mesh['pool'=2,'seq'=4,'head'=4] {'seq'}, dimensions={0}, use_global_device_ids=true | all-gather | bytes 983040 | tf_op jit(solution)/shard_map/all_gather | solution.py:135
  166.8 0.4 convolution_select_fusion
  167.2 5.2 %fusion.30 = f32[192,2048]{1,0:T(8,128)S(1)} fusion(bf16[192,2048]{1,0:T(8,128)(2,1)S(1)} %all_gather.11, bf16[2048,2048]{1,0:T(8,128)(2,1)} %param.25), kind=kOutput, calls=%fused_computation.53 | convolution fusion | flops 1610612736 | bytes 10747904 | tf_op jit(solution)/shard_map/dot_general | solution.py:138
  172.4 2.0 convolution_add_fusion
  174.5 0.2 convert_reduce_fusion
  174.7 29.9 %collective-permute-done = bf16[4,512,2,256]{3,1,2,0:T(8,128)(2,1)} collective-permute-done((bf16[4,512,2,256]{3,1,2,0:T(8,128)(2,1)S(1)}, bf16[4,512,2,256]{3,1,2,0:T(8,128)(2,1)}, u32[]{:S(2)}, u32[]{:S(2)}) %collective-permute-start) | collective-permute-done | bytes 2097184 | tf_op jit(solution)/shard_map/ppermute | solution.py:15
  204.6 5.1 %copy.71 = bf16[4,512,2,256]{3,2,1,0:T(2,128)(2,1)} copy(bf16[4,512,2,256]{3,1,2,0:T(8,128)(2,1)} %collective-permute-done) | data formatting | bytes 4194304 | tf_op jit(solution)/shard_map/ppermute | solution.py:15
  209.7 2.9 reshape.147
  212.6 3.7 %convolution_convert_fusion = bf16[2,4,262144]{2,1,0:T(4,128)(2,1)} fusion(bf16[4,262144,1]{1,0,2:T(4,128)(2,1)S(1)} %reshape.147, pred[4,4]{1,0:T(4,128)(4,1)S(1)} %iota_compare_fusion.2, pred[2,4]{1,0:T(4,128)(4,1)S(1)} %iota_compare_fusion.4), kind=kOutput, calls=%fused_computation | convolution fusion | flops 18874400 | bytes 6291480 | tf_op jit(solution)/shard_map/cdr,rx->cdx/dot_general | solution.py:64
  216.3 7.1 %reshape.136 = bf16[2,4,512,2,256]{4,3,2,1,0:T(2,128)(2,1)} reshape(bf16[2,4,262144]{2,1,0:T(4,128)(2,1)} %convolution_convert_fusion) | data formatting | bytes 8388608 | tf_op jit(solution)/shard_map/reshape | solution.py:65
  223.4 7.1 %copy.72 = bf16[2,4,512,2,256]{4,3,2,0,1:T(2,128)(2,1)} copy(bf16[2,4,512,2,256]{4,3,2,1,0:T(2,128)(2,1)} %reshape.136) | data formatting | bytes 8388608 | tf_op jit(solution)/shard_map/reshape | solution.py:65
  230.5 4.8 %all-to-all-start = ((bf16[2,4,512,2,256]{4,3,2,0,1:T(2,128)(2,1)}), bf16[2,4,512,2,256]{4,3,2,0,1:T(2,128)(2,1)}, u32[]{:S(2)}, u32[]{:S(2)}) async-start(bf16[2,4,512,2,256]{4,3,2,0,1:T(2,128)(2,1)} %copy.72), calls=%async_computation | async-start | bytes 8388608 | tf_op jit(solution)/shard_map/all_to_all | solution.py:125
  235.4 1.7 convert_element_type.50
  237.1 46.5 %all-to-all-done = bf16[2,4,512,2,256]{4,3,2,0,1:T(2,128)(2,1)} async-done(((bf16[2,4,512,2,256]{4,3,2,0,1:T(2,128)(2,1)}), bf16[2,4,512,2,256]{4,3,2,0,1:T(2,128)(2,1)}, u32[]{:S(2)}, u32[]{:S(2)}) %all-to-all-start) | async-done | bytes 4194336 | tf_op jit(solution)/shard_map/all_to_all | solution.py:125
  283.6 2.9 copy.73
  286.4 27.2 %copy.83 = bf16[1,2,2048,2,256]{4,3,2,1,0:T(2,128)(2,1)} copy(bf16[1,2,2048,2,256]{4,2,3,1,0:T(8,128)(2,1)S(1)} %bitcast.82) | data formatting | bytes 8388608
  (42 shorter events, 1.1 us)
Async XLA Ops:
  8.0 164.4 %copy-start = (bf16[8,16,2048]{2,1,0:T(8,128)(2,1)S(1)}, bf16[8,16,2048]{2,1,0:T(8,128)(2,1)}, u32[]{:S(2)}) copy-start(bf16[8,16,2048]{2,1,0:T(8,128)(2,1)} %param.27) | copy-start | bytes 1572868
  8.0 53.1 %all-gather.5.cloned.1.call-start = ((), (), s32[]{:S(2)}) async-start(), calls=%async_computation.3 | async-start | bytes 5242880 | tf_op jit(solution)/shard_map/all_gather | solution.py:90
  10.4 97.2 %all-gather.3.cloned.1.call-start = ((), (), s32[]{:S(2)}) async-start(), calls=%async_computation.2 | async-start | bytes 10485760 | tf_op jit(solution)/shard_map/all_gather | solution.py:89
  11.2 224.2 %reduce-scatter.2.cloned.1.call-start = ((), (), s32[]{:S(2)}) async-start(), calls=%async_computation.4 | async-start | bytes 1966080 | tf_op jit(solution)/shard_map/reduce_scatter | solution.py:140
  25.1 13.6 %copy-start.2 = (bf16[48,2048]{1,0:T(8,128)(2,1)S(1)}, bf16[48,2048]{1,0:T(8,128)(2,1)}, u32[]{:S(2)}) copy-start(bf16[48,2048]{1,0:T(8,128)(2,1)} %param.20) | copy-start | bytes 589828
  25.1 13.6 %copy-start.7 = (s32[48]{0:T(128)S(1)}, s32[48]{0:T(128)}, u32[]{:S(2)}) copy-start(s32[48]{0:T(128)} %param.23) | copy-start | bytes 580
  38.7 3.1 copy-start.4
  42.9 13.6 %copy-start.6 = (s32[4]{0:T(128)S(1)}, s32[4]{0:T(128)}, u32[]{:S(2)}) copy-start(s32[4]{0:T(128)} %param.18) | copy-start | bytes 52
  42.9 13.7 %copy-start.3 = (bf16[8,2,16,256]{3,2,1,0:T(8,128)(2,1)S(1)}, bf16[8,2,16,256]{3,2,1,0:T(8,128)(2,1)}, u32[]{:S(2)}) copy-start(bf16[8,2,16,256]{3,2,1,0:T(8,128)(2,1)} %param.17) | copy-start | bytes 393220
  152.7 14.1 %copy-start.1 = (bf16[2048,8,16]{0,2,1:T(8,128)(2,1)S(1)}, bf16[2048,8,16]{0,2,1:T(8,128)(2,1)}, u32[]{:S(2)}) copy-start(bf16[2048,8,16]{0,2,1:T(8,128)(2,1)} %param.26) | copy-start | bytes 1572868
  152.7 14.1 %copy-start.5 = (s32[192]{0:T(256)S(1)}, s32[192]{0:T(256)}, u32[]{:S(2)}) copy-start(s32[192]{0:T(256)} %param.24) | copy-start | bytes 2308
  156.7 47.9 %collective-permute-start = (bf16[4,512,2,256]{3,1,2,0:T(8,128)(2,1)S(1)}, bf16[4,512,2,256]{3,1,2,0:T(8,128)(2,1)}, u32[]{:S(2)}, u32[]{:S(2)}) collective-permute-start(bf16[4,512,2,256]{3,1,2,0:T(8,128)(2,1)S(1)} %fusion.5), channel_id=1, source_target_pairs={{0,16},{16,0},{1,17},{17,1},{2,18},{18,2},{3,19},{19,3},{4,20},{20... | collective-permute-start | bytes 6291464 | tf_op jit(solution)/shard_map/ppermute | solution.py:15
  172.4 2.0 copy-start.8
  230.5 53.0 %all-to-all-start = ((bf16[2,4,512,2,256]{4,3,2,0,1:T(2,128)(2,1)}), bf16[2,4,512,2,256]{4,3,2,0,1:T(2,128)(2,1)}, u32[]{:S(2)}, u32[]{:S(2)}) async-start(bf16[2,4,512,2,256]{4,3,2,0,1:T(2,128)(2,1)} %copy.72), calls=%async_computation | async-start | bytes 8388608 | tf_op jit(solution)/shard_map/all_to_all | solution.py:125
Sparse Core Ops, SparseCore 0:
  10.6 37.1 all-gather.4
  49.3 58.2 all-gather.2
Sparse Core Ops, SparseCore 1:
  174.5 34.7 reduce-scatter.1
where the time goes:
time: 323 us; the launch traced here: 321 us
  local copies, waits for them, and re-layouts  118 us (37%)
  waiting for transfers between devices  107 us (33%)
  matrix products  63.3 us (20%)
  between operations  15.7 us (5%)
  blocking collectives  8.55 us (3%)
  starting transfers between devices  6.5 us (2%)
    unnamed x24, local copies, waits for them, and re-layouts  56.8 us
    all_to_all x1, waiting for transfers between devices, body(): lax.all_to_all(outgoing, 'seq', split_axis=1, concat_axis=1, tiled=True)  46.5 us
    all_gather x1, waiting for transfers between devices, body(): weight_rows = lax.all_gather(key_value_weight, 'seq', axis=0, tiled=True)  29.9 us
    ppermute x1, waiting for transfers between devices, swapped(): return lax.ppermute(value, axis, pairs)  29.9 us
    dot_general x1, matrix products, body(): jnp.dot(token_matrix, weight_rows.reshape(decode_count, 2 * key_value_wid...  23.9 us
    reshape x1, local copies, waits for them, and re-layouts, body(): weight_rows.reshape(decode_count, 2 * key_value_width)  21.2 us
    dot_general x1, matrix products, body(): jnp.dot(token_matrix, lowered_rows, preferred_element_type=jnp.float32)  16.6 us
    reshape x2, local copies, waits for them, and re-layouts, place_slots(): outgoing.astype(jnp.bfloat16)  14.2 us
  transfers between devices with their start and end apart: 5, of which 3 were waited for; matrix products, arithmetic and copies ran while one was open for 32% of the time, Pallas kernels for 0%

commit v1 on v0

v1 whole, which is shorter than its diff:
```python
import jax
import jax.numpy as jnp
from jax import lax
from jax.experimental import pallas as pl
from jax.experimental.pallas import tpu as pltpu
from jax.sharding import PartitionSpec as P

HEAD_DIM = 128
ADAPTER_RANK = 16
ADAPTER_COUNT = 8
CAP = 2


def exchanged(value, axis, mask):
    pairs = [(source, source ^ mask) for source in range(lax.axis_size(axis))]
    return lax.ppermute(value, axis, pairs)


def gathered(value, axis):
    size = lax.axis_size(axis)
    index = lax.axis_index(axis)
    held = value[None]
    mask = size // 2
    while mask >= 1:
        other = exchanged(held, axis, mask)
        low_bit = (index // mask) % 2 == 0
        first = jnp.where(low_bit, held, other)
        second = jnp.where(low_bit, other, held)
        held = jnp.stack([first, second], axis=1).reshape((-1,) + value.shape)
        mask //= 2
    return held


def scattered_sum(value, axis):
    size = lax.axis_size(axis)
    index = lax.axis_index(axis)
    held = value.reshape((size, value.shape[0] // size) + value.shape[1:])
    mask = 1
    while mask < size:
        split = held.reshape((held.shape[0] // 2, 2) + held.shape[1:])
        low_bit = (index // mask) % 2 == 0
        keep = jnp.where(low_bit, split[:, 0], split[:, 1])
        give = jnp.where(low_bit, split[:, 1], split[:, 0])
        held = keep + exchanged(give, axis, mask)
        mask *= 2
    return held[0]


def attend_kernel(lengths, query_ref, cache_ref, key_ref, value_ref, out_ref):
    rows, positions = cache_ref.shape[0], cache_ref.shape[1]
    kv_heads = key_ref.shape[1]
    groups = query_ref.shape[1] // kv_heads
    start = pl.program_id(0) * rows
    lane = lax.broadcasted_iota(jnp.int32, (groups, 2 * positions), 1)
    factor = HEAD_DIM ** (-0.5)
    for row in range(rows):
        pairs = cache_ref[row].reshape(2 * positions, kv_heads * HEAD_DIM)
        length = lengths[start + row]
        valid = (lane % 2 == 0) & (lane < 2 * length)
        for head in range(kv_heads):
            block = pairs[:, head * HEAD_DIM : (head + 1) * HEAD_DIM]
            query = query_ref[row, head * groups : (head + 1) * groups, :]
            own_key = key_ref[row, head : head + 1, :].astype(jnp.float32)
            own_value = value_ref[row, head : head + 1, :].astype(jnp.float32)
            scores = (
                lax.dot_general(
                    query, block, (((1,), (1,)), ((), ())), preferred_element_type=jnp.float32
                )
                * factor
            )
            own = jnp.sum(query.astype(jnp.float32) * own_key, axis=1, keepdims=True) * factor
            highest = jnp.maximum(
                jnp.max(jnp.where(valid, scores, -1e30), axis=1, keepdims=True), own
            )
            raw = jnp.where(valid, jnp.exp(scores - highest), 0.0)
            own_raw = jnp.exp(own - highest)
            total = jnp.sum(raw, axis=1, keepdims=True) + own_raw
            weights = pltpu.roll(raw / total, 1, 1).astype(jnp.bfloat16)
            own_weight = (own_raw / total).astype(jnp.bfloat16).astype(jnp.float32)
            mixed = jnp.dot(weights, block, preferred_element_type=jnp.float32)
            out_ref[row, head * groups : (head + 1) * groups, :] = (
                mixed + own_weight * own_value
            ).astype(jnp.bfloat16)


def attend(query, cache, current, lengths):
    rows, positions, _, width = cache.shape
    kv_heads = width // HEAD_DIM
    heads = query.shape[1] // HEAD_DIM
    step = next(size for size in (8, 4, 2, 1) if rows % size == 0)
    query = query.reshape(rows, heads, HEAD_DIM)
    own_key = current[:, 0].reshape(rows, kv_heads, HEAD_DIM)
    own_value = current[:, 1].reshape(rows, kv_heads, HEAD_DIM)
    out = pl.pallas_call(
        attend_kernel,
        grid_spec=pltpu.PrefetchScalarGridSpec(
            num_scalar_prefetch=1,
            grid=(rows // step,),
            in_specs=[
                pl.BlockSpec((step, heads, HEAD_DIM), lambda i, _: (i, 0, 0)),
                pl.BlockSpec((step, positions, 2, width), lambda i, _: (i, 0, 0, 0)),
                pl.BlockSpec((step, kv_heads, HEAD_DIM), lambda i, _: (i, 0, 0)),
                pl.BlockSpec((step, kv_heads, HEAD_DIM), lambda i, _: (i, 0, 0)),
            ],
            out_specs=pl.BlockSpec((step, heads, HEAD_DIM), lambda i, _: (i, 0, 0)),
        ),
        out_shape=jax.ShapeDtypeStruct((rows, heads, HEAD_DIM), jnp.bfloat16),
        cost_estimate=pl.CostEstimate(
            flops=8 * rows * heads * positions * HEAD_DIM,
            bytes_accessed=4 * rows * positions * width,
            transcendentals=2 * rows * heads * positions,
        ),
    )(lengths, query, cache, own_key, own_value)
    return out.reshape(rows, heads * HEAD_DIM)


def weave_kernel(key_ref, value_ref, out_ref):
    tokens, width = key_ref.shape[2], key_ref.shape[3]
    part = 128
    row = lax.broadcasted_iota(jnp.int32, (2 * part, 2 * part), 0)
    column = lax.broadcasted_iota(jnp.int32, (2 * part, 2 * part), 1)
    order = jnp.where(column == (row % 2) * part + row // 2, 1.0, 0.0).astype(jnp.bfloat16)
    for at in range(0, tokens, part):
        both = jnp.concatenate(
            [key_ref[0, 0, at : at + part, :], value_ref[0, 0, at : at + part, :]], axis=0
        )
        woven = jnp.dot(order, both, preferred_element_type=jnp.float32).astype(jnp.bfloat16)
        out_ref[0, 0, at : at + part, :, :] = woven.reshape(part, 2, width)


def weave(keys, values):
    sources, slots, tokens, width = keys.shape
    spec = pl.BlockSpec((1, 1, tokens, width), lambda slot, source: (source, slot, 0, 0))
    return pl.pallas_call(
        weave_kernel,
        grid=(slots, sources),
        in_specs=[spec, spec],
        out_specs=pl.BlockSpec(
            (1, 1, tokens, 2, width), lambda slot, source: (0, slot, source, 0, 0)
        ),
        out_shape=jax.ShapeDtypeStruct((1, slots, sources * tokens, 2, width), jnp.bfloat16),
        cost_estimate=pl.CostEstimate(
            flops=1024 * slots * sources * tokens * width,
            bytes_accessed=8 * slots * sources * tokens * width,
            transcendentals=0,
        ),
    )(keys, values)


def slot_hits(owners, decoders):
    requests = owners.shape[0]
    order = jnp.arange(requests, dtype=jnp.int32)
    same = owners[:, None] == owners[None, :]
    slot_of = jnp.sum((same & (order[None, :] < order[:, None])).astype(jnp.int32), axis=1)
    slot_hit = slot_of[None, :] == jnp.arange(CAP, dtype=jnp.int32)[:, None]
    owner_hit = owners[None, :] == jnp.arange(decoders, dtype=jnp.int32)[:, None]
    return owner_hit[:, None, :] & slot_hit[None, :, :]


def hand_over(block, hits):
    arrived = exchanged(block, "pool", 1)
    outgoing = jnp.zeros(hits.shape[:2] + block.shape[1:], block.dtype)
    for request in range(block.shape[0]):
        outgoing = jnp.where(
            hits[:, :, request][:, :, None, None], arrived[request][None, None], outgoing
        )
    return lax.all_to_all(outgoing, "seq", split_axis=0, concat_axis=0, tiled=True)


def body(
    prompt,
    key_value_weight,
    adapter_down_weight,
    adapter_up_weight,
    request_adapter_index,
    destination,
    rotated_query,
    key_value_cache,
    current_key_value,
    cached_length,
    row_adapter_index,
    output_weight,
    output_down_weight,
    output_up_weight,
):
    requests, tok_dev, model_width = prompt.shape
    width = key_value_weight.shape[2]
    shard = key_value_weight.shape[0]
    decoders = lax.axis_size("seq")
    heads = lax.axis_size("head")
    columns = 2 * ADAPTER_RANK
    tokens = prompt.reshape(requests * tok_dev, model_width)

    share = requests // heads if requests % heads == 0 else requests
    mine = lax.axis_index("head") * share if share < requests else 0
    my_adapter = lax.dynamic_slice_in_dim(request_adapter_index, mine, share)
    column = jnp.arange(ADAPTER_COUNT * columns, dtype=jnp.int32)
    wanted = my_adapter[:, None] * columns + jnp.arange(columns, dtype=jnp.int32)[None, :]
    pick = (wanted.reshape(-1)[:, None] == column[None, :]).astype(jnp.bfloat16)
    down = lax.dot_general(
        pick, adapter_down_weight, (((1,), (1,)), ((), ())), preferred_element_type=jnp.float32
    ).astype(jnp.bfloat16)
    matrix = key_value_weight.reshape(shard, 2 * width)
    down_all = gathered(down, "seq")
    key_all = gathered(matrix[:, :width], "seq").reshape(model_width, width)
    value_all = gathered(matrix[:, width:], "seq").reshape(model_width, width)

    attended = attend(rotated_query, key_value_cache, current_key_value, cached_length)
    attn_rows = gathered(attended, "seq").reshape(-1, attended.shape[1])
    ranks = ADAPTER_COUNT * ADAPTER_RANK
    down_flat = output_down_weight.reshape(output_down_weight.shape[0], ranks)
    up_flat = output_up_weight.reshape(ranks, output_up_weight.shape[2])
    rank_owner = jnp.arange(ranks, dtype=jnp.int32) // ADAPTER_RANK
    low_rows = jnp.dot(attn_rows, down_flat, preferred_element_type=jnp.float32)
    low_rows = jnp.where(row_adapter_index[:, None] == rank_owner[None, :], low_rows, 0.0)
    terms = jnp.dot(attn_rows, output_weight, preferred_element_type=jnp.float32)
    terms = terms + jnp.dot(
        low_rows.astype(jnp.bfloat16), up_flat, preferred_element_type=jnp.float32
    )
    decoded = scattered_sum(terms, "head").astype(jnp.bfloat16)

    my_tokens = lax.dynamic_slice_in_dim(prompt, mine, share, axis=0)
    my_down = down_all.transpose(1, 0, 2).reshape(share, columns, model_width)
    my_low = jnp.einsum("rtk,rck->rct", my_tokens, my_down, preferred_element_type=jnp.float32)
    low = gathered(my_low, "head") if share < requests else my_low[None]
    low = low.reshape(requests, 2, ADAPTER_RANK, tok_dev).astype(jnp.bfloat16)
    own = jnp.eye(requests, dtype=jnp.bool_)[None, :, None, :, None]
    spread = jnp.where(
        own, low.transpose(1, 0, 2, 3)[:, :, :, None, :], jnp.zeros((), jnp.bfloat16)
    ).reshape(2, requests * ADAPTER_RANK, requests * tok_dev)
    selector = request_adapter_index[:, None] == jnp.arange(ADAPTER_COUNT, dtype=jnp.int32)[None, :]
    up = jnp.einsum(
        "um,mdzt->duzt",
        selector.astype(jnp.bfloat16),
        adapter_up_weight,
        preferred_element_type=jnp.float32,
    ).astype(jnp.bfloat16)
    up = up.reshape(2, requests * ADAPTER_RANK, width)

    pool_index = lax.axis_index("pool")
    other_owners = lax.dynamic_slice_in_dim(destination, (1 - pool_index) * requests, requests)
    hits = slot_hits(other_owners, decoders)

    handed = []
    for which, weight in enumerate((key_all, value_all)):
        base = jnp.dot(tokens, weight, preferred_element_type=jnp.float32)
        extra = lax.dot_general(
            spread[which], up[which], (((0,), (0,)), ((), ())), preferred_element_type=jnp.float32
        )
        block = (base + extra).astype(jnp.bfloat16).reshape(requests, tok_dev, width)
        handed.append(hand_over(block, hits))
    return (weave(handed[0], handed[1]), decoded)


def solution(mesh):
    in_specs = (
        P("pool", "seq", None),
        P("seq", None, "head"),
        P("seq", None),
        P(None, None, None, "head"),
        P("pool"),
        P(),
        P(("pool", "seq"), "head"),
        P(("pool", "seq"), None, None, "head"),
        P(("pool", "seq"), None, "head"),
        P(("pool", "seq")),
        P("pool"),
        P("head", "seq"),
        P("head", None, None),
        P(None, None, "seq"),
    )
    out_specs = (P(("pool", "seq"), None, None, None, "head"), P(("pool", "head"), "seq"))
    return jax.shard_map(body, mesh=mesh, in_specs=in_specs, out_specs=out_specs, check_vma=False)
```

time: 323 us -> 224 us (0.69)
  local copies, waits for them, and re-layouts: 118 us -> 15.5 us
  Pallas kernels: 0 us -> 48.5 us
  waiting for transfers between devices: 107 us -> 67.3 us
  starting transfers between devices: 6.5 us -> 25 us
  between operations: 15.7 us -> 1.77 us
  matrix products: 63.3 us -> 50.6 us
  other arithmetic: 2.48 us -> 14.7 us
  blocking collectives: 8.55 us -> 0 us
    unnamed x24 -> x34, local copies, waits for them, and re-layouts: 56.8 us -> 3.7 us
    pallas_call x0 -> x2, Pallas kernels: none -> 48.5 us  [the longest x1 40.9 us: attend(): pl.pallas_call(attend_kernel, grid_spec=pltpu.PrefetchScalarGridSpec(num_...]
    reshape x4 -> x2, local copies, waits for them, and re-layouts: 38.3 us -> 2.62 us  [body(): (base + extra).astype(jnp.bfloat16).reshape(requests, tok_dev, width)]
    all_gather x2 -> x0, waiting for transfers between devices: 29.9 us -> none  [the longest x1 29.9 us: body(): weight_rows = lax.all_gather(key_value_weight, 'seq', axis=0, tiled=True)]
    all_to_all x1 -> x2, waiting for transfers between devices: 46.5 us -> 25.3 us  [hand_over(): lax.all_to_all(outgoing, 'seq', split_axis=0, concat_axis=0, tiled=True)]
    ppermute x1 -> x14, starting transfers between devices: 1.54 us -> 15.9 us  [exchanged(): return lax.ppermute(value, axis, pairs)]
    dot_general x10 -> x8, matrix products: 58.1 us -> 44.2 us  [the longest x2 32.4 us: body(): base = jnp.dot(tokens, weight, preferred_element_type=jnp.float32)]
    slice x1 -> x5, local copies, waits for them, and re-layouts: 13.9 us -> 1.04 us  [the longest x3 0.65 us: body(): up[which]]
  transfers between devices with their start and end apart: 5 -> 16, of which waited for: 3 -> 7; matrix products, arithmetic and copies ran while one was open for 32% -> 33% of each run, Pallas kernels for 0% -> 18%
where the time goes in v1:
time: 224 us; the launch traced here: 223 us
  waiting for transfers between devices  67.3 us (30%)
  matrix products  50.6 us (23%)
  Pallas kernels  48.5 us (22%)
  starting transfers between devices  25 us (11%)
  local copies, waits for them, and re-layouts  15.5 us (7%)
  other arithmetic  14.7 us (7%)
    ppermute x14, waiting for transfers between devices, exchanged(): return lax.ppermute(value, axis, pairs)  42 us
    pallas_call x1, Pallas kernels, attend(): pl.pallas_call(attend_kernel, grid_spec=pltpu.PrefetchScalarGridSpec(num_...  40.9 us
    dot_general x2, matrix products, body(): base = jnp.dot(tokens, weight, preferred_element_type=jnp.float32)  32.4 us
    all_to_all x2, waiting for transfers between devices, hand_over(): lax.all_to_all(outgoing, 'seq', split_axis=0, concat_axis=0, tiled=True)  25.3 us
    ppermute x14, starting transfers between devices, exchanged(): return lax.ppermute(value, axis, pairs)  15.9 us
    all_to_all x2, starting transfers between devices, hand_over(): lax.all_to_all(outgoing, 'seq', split_axis=0, concat_axis=0, tiled=True)  9.05 us
    another operation x14, other arithmetic, gathered(): held = jnp.stack([first, second], axis=1).reshape((-1,) + value.shape)  7.78 us
    pallas_call x1, Pallas kernels, weave(): pl.pallas_call(weave_kernel, grid=(slots, sources), in_specs=[spec, spec]...  7.61 us
  transfers between devices with their start and end apart: 16, of which 7 were waited for; matrix products, arithmetic and copies ran while one was open for 33% of the time, Pallas kernels for 18%

profile of v1, /device:TPU:0, one launch (start us, length us, event | category | flops | bytes accessed | tf_op | source)
XLA Modules:
  0.0 223.3 jit_solution(14662557767714921723)
XLA Ops:
  0.6 2.1 copy.47
  2.8 1.5 slice_bitcast_fusion
  4.3 3.0 %collective-permute-start.7 = (bf16[1,2048,256]{2,1,0:T(8,128)(2,1)}, bf16[1,2048,256]{2,1,0:T(8,128)(2,1)}, u32[]{:S(2)}, u32[]{:S(2)}) collective-permute-start(bf16[1,2048,256]{2,1,0:T(8,128)(2,1)} %get-tuple-element.14), channel_id=1, source_target_pairs={{0,8},{4,12},{8,0},{12,4},{1,9},{5,13},{9,1},{13,5},{2,10},{6,14},... | collective-permute-start | bytes 3145736 | tf_op jit(solution)/shard_map/ppermute | solution.py:16
  9.0 2.0 collective-permute-start.2
  13.2 40.9 %shard_map.150 = bf16[48,16,128]{2,1,0:T(8,128)(2,1)} custom-call(s32[48]{0:T(128)} %lengths.1, bf16[48,16,128]{2,1,0:T(8,128)(2,1)} %bitcast.224, bf16[48,128,2,256]{3,2,1,0:T(2,128)(2,1)} %cache_ref.1, bf16[48,2,128]{2,1,0:T(2,128)(2,1)} %reshape_squeeze.6.key_ref, bf16[48,2,128]{2,1,0:T(2,128)(2,1)} %reshape_squeeze.7.value_ref), custom_call_target="tpu_custom_call" | custom-call | flops 100663296 | bytes 6291456 | tf_op jit(solution)/shard_map/pallas_call | solution.py:94
  57.2 3.7 %collective-permute-done.10 = bf16[1,48,2048]{2,1,0:T(8,128)(2,1)S(1)} collective-permute-done((bf16[1,48,2048]{2,1,0:T(8,128)(2,1)S(1)}, bf16[1,48,2048]{2,1,0:T(8,128)(2,1)S(1)}, u32[]{:S(2)}, u32[]{:S(2)}) %collective-permute-start.10) | collective-permute-done | bytes 196640 | tf_op jit(solution)/shard_map/ppermute | solution.py:16
  61.2 6.0 %fusion.8 = bf16[1,1,32,512]{3,2,1,0:T(8,128)(2,1)S(1)} fusion(bf16[32,8192]{1,0:T(8,128)(2,1)S(1)} %bitcast.213, bf16[4,512,8192]{2,1,0:T(8,128)(2,1)} %param.14, s32[]{:T(128)S(6)} %select_n.282), kind=kOutput, calls=%fused_computation.26 | convolution fusion | flops 268435456 | bytes 8945668 | tf_op jit(solution)/shard_map/rtk,rck->rct/dot_general | solution.py:224
  67.2 2.6 %collective-permute-start.4 = (bf16[1,1,32,512]{3,2,1,0:T(8,128)(2,1)S(1)}, bf16[1,1,32,512]{3,2,1,0:T(8,128)(2,1)S(1)}, u32[]{:S(2)}, u32[]{:S(2)}) collective-permute-start(bf16[1,1,32,512]{3,2,1,0:T(8,128)(2,1)S(1)} %fusion.8), channel_id=1, source_target_pairs={{0,2},{1,3},{2,0},{3,1},{4,6},{5,7},{6,4},{7,5},{8,10},{9,11},{10,... | collective-permute-start | bytes 98312 | tf_op jit(solution)/shard_map/ppermute | solution.py:16
  69.8 1.8 select_bitcast_fusion.5
  72.0 1.6 collective-permute-start.5
  73.9 2.6 %collective-permute-done.5 = bf16[2,1,32,512]{3,2,0,1:T(8,128)(2,1)S(1)} collective-permute-done((bf16[2,1,32,512]{3,2,0,1:T(8,128)(2,1)S(1)}, bf16[2,1,32,512]{3,2,0,1:T(8,128)(2,1)S(1)}, u32[]{:S(2)}, u32[]{:S(2)}) %collective-permute-start.5) | collective-permute-done | bytes 65568 | tf_op jit(solution)/shard_map/ppermute | solution.py:16
  78.6 1.5 maximum_bitcast_fusion
  80.8 2.3 %copy.32 = bf16[2,2,2048,256]{3,2,1,0:T(8,128)(2,1)} copy(bf16[2,2,2048,256]{3,2,0,1:T(8,128)(2,1)S(1)} %pad_maximum_fusion.1) | data formatting | bytes 8388608 | tf_op jit(solution)/shard_map/stack | solution.py:29
  83.1 16.9 %convolution_bitcast_fusion = f32[2048,256]{0,1:T(8,128)} fusion(bf16[8192,256]{1,0:T(8,128)(2,1)} %bitcast.210, bf16[2048,8192]{1,0:T(8,128)(2,1)} %bitcast.214), kind=kOutput, calls=%fused_computation.6 | convolution fusion | flops 8589934592 | bytes 39845888 | tf_op jit(solution)/shard_map/dot_general | solution.py:246
  100.1 2.1 fusion.4
  102.2 1.3 copy.43
  103.5 1.5 collective-permute-start.9
  105.0 1.9 select_bitcast_fusion.3
  106.9 2.4 %pad_maximum_fusion = bf16[2,2,2048,256]{3,2,1,0:T(8,128)(2,1)} fusion(bf16[2,1,2048,256]{3,2,1,0:T(8,128)(2,1)S(1)} %get-tuple-element.7, bf16[2,1,2048,256]{3,2,1,0:T(8,128)(2,1)S(1)} %get-tuple-element.6), kind=kLoop, calls=%fused_computation.3 | loop fusion | flops 2097152 | bytes 8388608 | tf_op jit(solution)/shard_map/stack | solution.py:29
  109.3 15.4 %convolution_bitcast_fusion.1 = f32[2048,256]{0,1:T(8,128)S(1)} fusion(bf16[8192,256]{1,0:T(8,128)(2,1)} %bitcast.209, bf16[2048,8192]{1,0:T(8,128)(2,1)} %bitcast.215), kind=kOutput, calls=%fused_computation.8 | convolution fusion | flops 8589934592 | bytes 39845888 | tf_op jit(solution)/shard_map/dot_general | solution.py:246
  127.2 6.4 %fusion.30 = f32[192,2048]{1,0:T(8,128)} fusion(bf16[192,2048]{1,0:T(8,128)(2,1)S(1)} %bitcast.211, bf16[2048,2048]{1,0:T(8,128)(2,1)} %param.25), kind=kOutput, calls=%fused_computation.103 | convolution fusion | flops 1610612736 | bytes 10747904 | tf_op jit(solution)/shard_map/dot_general | solution.py:216
  134.8 17.3 %collective-permute-done.6 = bf16[4,512,256]{2,1,0:T(8,128)(2,1)S(1)} collective-permute-done((bf16[4,512,256]{2,1,0:T(8,128)(2,1)}, bf16[4,512,256]{2,1,0:T(8,128)(2,1)S(1)}, u32[]{:S(2)}, u32[]{:S(2)}) %collective-permute-start.6) | collective-permute-done | bytes 1048608 | tf_op jit(solution)/shard_map/ppermute | solution.py:16
  152.1 3.0 %select_select_fusion = (bf16[4,2,512,256]{3,2,1,0:T(8,128)(2,1)}, bf16[4,2,512,256]{3,2,1,0:T(8,128)(2,1)}) fusion(pred[4,2]{1,0:T(4,128)(4,1)S(1)} %get-tuple-element.43, pred[4,2]{1,0:T(4,128)(4,1)S(1)} %get-tuple-element.44, pred[4,2]{1,0:T(4,128)(4,1)S(1)} %get-tuple-element.45, pred[4,2]{1,0:T(4,128)(4,1)S(1)} %get-tuple-element.42, ...), kind=kLoop, calls=%fused_computation.16 | loop fusion | flops 8388608 | bytes 6291488 | tf_op jit(solution)/shard_map/jit(_where)/select_n | solution.py:164
  155.1 4.6 %all-to-all-start = ((bf16[4,2,512,256]{3,2,1,0:T(8,128)(2,1)}), bf16[4,2,512,256]{3,2,1,0:T(8,128)(2,1)}, u32[]{:S(2)}, u32[]{:S(2)}) async-start(bf16[4,2,512,256]{3,2,1,0:T(8,128)(2,1)} %get-tuple-element.41), calls=%async_computation | async-start | bytes 4194304 | tf_op jit(solution)/shard_map/all_to_all | solution.py:167
  159.8 2.6 %convolution_add_fusion.2 = f32[192,2048]{1,0:T(8,128)S(1)} fusion(f32[192,2048]{1,0:T(8,128)} %fusion.30, bf16[128,2048]{1,0:T(8,128)(2,1)S(1)} %bitcast.225, bf16[192,2048]{1,0:T(8,128)(2,1)S(1)} %bitcast.212, bf16[2048,128]{0,1:T(8,128)(2,1)} %bitcast.226, s32[128]{0:T(128)S(1)} %copy-done.13, s32[192]{0:T(256)S(1)} %copy-done.11), kind=kOutput, calls=%fused_computation.11 | convolution fusion | flops 201793536 | bytes 4982016 | tf_op jit(solution)/shard_map/dot_general | solution.py:217
  162.5 1.6 collective-permute-start.12
  164.1 21.3 %all-to-all-done.key_ref = bf16[4,2,512,256]{3,2,1,0:T(8,128)(2,1)} async-done(((bf16[4,2,512,256]{3,2,1,0:T(8,128)(2,1)}), bf16[4,2,512,256]{3,2,1,0:T(8,128)(2,1)}, u32[]{:S(2)}, u32[]{:S(2)}) %all-to-all-start) | async-done | bytes 2097184 | tf_op jit(solution)/shard_map/all_to_all | solution.py:167
  185.5 4.5 %all-to-all-start.1 = ((bf16[4,2,512,256]{3,2,1,0:T(8,128)(2,1)}), bf16[4,2,512,256]{3,2,1,0:T(8,128)(2,1)}, u32[]{:S(2)}, u32[]{:S(2)}) async-start(bf16[4,2,512,256]{3,2,1,0:T(8,128)(2,1)} %get-tuple-element.40), calls=%async_computation.1 | async-start | bytes 4194304 | tf_op jit(solution)/shard_map/all_to_all | solution.py:167
  190.1 2.6 %collective-permute-start.13 = (f32[1,48,2048]{2,1,0:T(8,128)S(1)}, f32[1,48,2048]{2,1,0:T(8,128)S(1)}, u32[]{:S(2)}, u32[]{:S(2)}) collective-permute-start(f32[1,48,2048]{2,1,0:T(8,128)S(1)} %select_bitcast_fusion.9), channel_id=1, source_target_pairs={{0,2},{1,3},{2,0},{3,1},{4,6},{5,7},{6,4},{7,5},{8,10},{9,11},{10,... | collective-permute-start | bytes 1179656 | tf_op jit(solution)/shard_map/ppermute | solution.py:16
  192.7 18.3 %collective-permute-done.13 = f32[1,48,2048]{2,1,0:T(8,128)S(1)} collective-permute-done((f32[1,48,2048]{2,1,0:T(8,128)S(1)}, f32[1,48,2048]{2,1,0:T(8,128)S(1)}, u32[]{:S(2)}, u32[]{:S(2)}) %collective-permute-start.13) | collective-permute-done | bytes 393248 | tf_op jit(solution)/shard_map/ppermute | solution.py:16
  211.7 3.9 %all-to-all-done.1.value_ref = bf16[4,2,512,256]{3,2,1,0:T(8,128)(2,1)} async-done(((bf16[4,2,512,256]{3,2,1,0:T(8,128)(2,1)}), bf16[4,2,512,256]{3,2,1,0:T(8,128)(2,1)}, u32[]{:S(2)}, u32[]{:S(2)}) %all-to-all-start.1) | async-done | bytes 2097184 | tf_op jit(solution)/shard_map/all_to_all | solution.py:167
  215.7 7.6 %shard_map.149 = bf16[1,2,2048,2,256]{4,3,2,1,0:T(2,128)(2,1)} custom-call(bf16[4,2,512,256]{3,2,1,0:T(8,128)(2,1)} %all-to-all-done.key_ref, bf16[4,2,512,256]{3,2,1,0:T(8,128)(2,1)} %all-to-all-done.1.value_ref), custom_call_target="tpu_custom_call" | custom-call | flops 1073741824 | bytes 8388608 | tf_op jit(solution)/shard_map/pallas_call | solution.py:134
  (97 shorter events, 14.6 us)
Async XLA Ops:
  0.6 7.9 %copy-start = (bf16[2048,256]{1,0:T(8,128)(2,1)S(1)}, bf16[2048,256]{1,0:T(8,128)(2,1)}, u32[]{:S(2)}) copy-start(bf16[2048,256]{1,0:T(8,128)(2,1)} %param.16) | copy-start | bytes 3145732
  2.8 4.5 %copy-start.12 = (s32[4]{0:T(128)S(1)}, s32[4]{0:T(128)}, u32[]{:S(2)}) copy-start(s32[4]{0:T(128)} %param.18) | copy-start | bytes 52
  2.8 8.2 %copy-start.7 = (bf16[48,2048]{1,0:T(8,128)(2,1)S(1)}, bf16[48,2048]{1,0:T(8,128)(2,1)}, u32[]{:S(2)}) copy-start(bf16[48,2048]{1,0:T(8,128)(2,1)} %param.20) | copy-start | bytes 589828
  2.8 8.9 %copy-start.8 = (bf16[48,2,256]{2,1,0:T(2,128)(2,1)S(1)}, bf16[48,2,256]{2,1,0:T(2,128)(2,1)}, u32[]{:S(2)}) copy-start(bf16[48,2,256]{2,1,0:T(2,128)(2,1)} %param.22) | copy-start | bytes 147460
  4.3 65.5 %collective-permute-start.7 = (bf16[1,2048,256]{2,1,0:T(8,128)(2,1)}, bf16[1,2048,256]{2,1,0:T(8,128)(2,1)}, u32[]{:S(2)}, u32[]{:S(2)}) collective-permute-start(bf16[1,2048,256]{2,1,0:T(8,128)(2,1)} %get-tuple-element.14), channel_id=1, source_target_pairs={{0,8},{4,12},{8,0},{12,4},{1,9},{5,13},{9,1},{13,5},{2,10},{6,14},... | collective-permute-start | bytes 3145736 | tf_op jit(solution)/shard_map/ppermute | solution.py:16
  7.3 62.5 %collective-permute-start = (bf16[1,2048,256]{2,1,0:T(8,128)(2,1)}, bf16[1,2048,256]{2,1,0:T(8,128)(2,1)}, u32[]{:S(2)}, u32[]{:S(2)}) collective-permute-start(bf16[1,2048,256]{2,1,0:T(8,128)(2,1)} %get-tuple-element.15), channel_id=1, source_target_pairs={{0,8},{4,12},{8,0},{12,4},{1,9},{5,13},{9,1},{13,5},{2,10},{6,14},... | collective-permute-start | bytes 3145736 | tf_op jit(solution)/shard_map/ppermute | solution.py:16
  9.0 48.1 %collective-permute-start.2 = (bf16[1,32,2048]{2,1,0:T(8,128)(2,1)S(1)}, bf16[1,32,2048]{2,1,0:T(8,128)(2,1)S(1)}, u32[]{:S(2)}, u32[]{:S(2)}) collective-permute-start(bf16[1,32,2048]{2,1,0:T(8,128)(2,1)S(1)} %fusion.5), channel_id=1, source_target_pairs={{0,8},{4,12},{8,0},{12,4},{1,9},{5,13},{9,1},{13,5},{2,10},{6,14},... | collective-permute-start | bytes 393224 | tf_op jit(solution)/shard_map/ppermute | solution.py:16
  13.2 42.0 %copy-start.14 = (s32[8]{0:T(128)S(1)}, s32[8]{0:T(128)}, u32[]{:S(2)}) copy-start(s32[8]{0:T(128)} %param.19) | copy-start | bytes 100
  13.2 42.4 %copy-start.10 = (bf16[8,2,16,256]{3,2,1,0:T(8,128)(2,1)S(1)}, bf16[8,2,16,256]{3,2,1,0:T(8,128)(2,1)}, u32[]{:S(2)}) copy-start(bf16[8,2,16,256]{3,2,1,0:T(8,128)(2,1)} %param.17) | copy-start | bytes 393220
  55.1 5.9 %collective-permute-start.10 = (bf16[1,48,2048]{2,1,0:T(8,128)(2,1)S(1)}, bf16[1,48,2048]{2,1,0:T(8,128)(2,1)S(1)}, u32[]{:S(2)}, u32[]{:S(2)}) collective-permute-start(bf16[1,48,2048]{2,1,0:T(8,128)(2,1)S(1)} %broadcast_in_dim_reshape.4), channel_id=1, source_target_pairs={{0,8},{4,12},{8,0},{12,4},{1,9},{5,13},{9,1},{13,5},{2,10},{6,14},... | collective-permute-start | bytes 589832 | tf_op jit(solution)/shard_map/ppermute | solution.py:16
  57.1 3.8 %collective-permute-start.3 = (bf16[2,32,2048]{2,1,0:T(8,128)(2,1)S(1)}, bf16[2,32,2048]{2,1,0:T(8,128)(2,1)S(1)}, u32[]{:S(2)}, u32[]{:S(2)}) collective-permute-start(bf16[2,32,2048]{2,1,0:T(8,128)(2,1)S(1)} %maximum_bitcast_fusion.3), channel_id=1, source_target_pairs={{0,4},{4,0},{8,12},{12,8},{1,5},{5,1},{9,13},{13,9},{2,6},{6,2},{1... | collective-permute-start | bytes 786440 | tf_op jit(solution)/shard_map/ppermute | solution.py:16
  67.2 4.8 %collective-permute-start.4 = (bf16[1,1,32,512]{3,2,1,0:T(8,128)(2,1)S(1)}, bf16[1,1,32,512]{3,2,1,0:T(8,128)(2,1)S(1)}, u32[]{:S(2)}, u32[]{:S(2)}) collective-permute-start(bf16[1,1,32,512]{3,2,1,0:T(8,128)(2,1)S(1)} %fusion.8), channel_id=1, source_target_pairs={{0,2},{1,3},{2,0},{3,1},{4,6},{5,7},{6,4},{7,5},{8,10},{9,11},{10,... | collective-permute-start | bytes 98312 | tf_op jit(solution)/shard_map/ppermute | solution.py:16
  71.6 7.0 %copy-start.2 = (bf16[1,1,2048,256]{3,2,1,0:T(8,128)(2,1)}, bf16[1,1,2048,256]{3,2,1,0:T(8,128)(2,1)S(1)}, u32[]{:S(2)}) copy-start(bf16[1,1,2048,256]{3,2,1,0:T(8,128)(2,1)S(1)} %get-tuple-element.13) | copy-start | bytes 3145732
  71.8 8.4 %collective-permute-start.8 = (bf16[2,2048,256]{2,1,0:T(8,128)(2,1)S(1)}, bf16[2,2048,256]{2,1,0:T(8,128)(2,1)S(1)}, u32[]{:S(2)}, u32[]{:S(2)}) collective-permute-start(bf16[2,2048,256]{2,1,0:T(8,128)(2,1)S(1)} %maximum_bitcast_fusion.1), channel_id=1, source_target_pairs={{0,4},{4,0},{8,12},{12,8},{1,5},{5,1},{9,13},{13,9},{2,6},{6,2},{1... | collective-permute-start | bytes 6291464 | tf_op jit(solution)/shard_map/ppermute | solution.py:16
  72.0 4.5 %collective-permute-start.5 = (bf16[2,1,32,512]{3,2,0,1:T(8,128)(2,1)S(1)}, bf16[2,1,32,512]{3,2,0,1:T(8,128)(2,1)S(1)}, u32[]{:S(2)}, u32[]{:S(2)}) collective-permute-start(bf16[2,1,32,512]{3,2,0,1:T(8,128)(2,1)S(1)} %maximum_bitcast_fusion.4), channel_id=1, source_target_pairs={{0,1},{1,0},{2,3},{3,2},{4,5},{5,4},{6,7},{7,6},{8,9},{9,8},{10,11... | collective-permute-start | bytes 196616 | tf_op jit(solution)/shard_map/ppermute | solution.py:16
  73.7 4.1 %collective-permute-start.11 = (bf16[2,48,2048]{2,1,0:T(8,128)(2,1)S(1)}, bf16[2,48,2048]{2,1,0:T(8,128)(2,1)S(1)}, u32[]{:S(2)}, u32[]{:S(2)}) collective-permute-start(bf16[2,48,2048]{2,1,0:T(8,128)(2,1)S(1)} %maximum_bitcast_fusion.2), channel_id=1, source_target_pairs={{0,4},{4,0},{8,12},{12,8},{1,5},{5,1},{9,13},{13,9},{2,6},{6,2},{1... | collective-permute-start | bytes 1179656 | tf_op jit(solution)/shard_map/ppermute | solution.py:16
  80.2 24.9 %collective-permute-start.1 = (bf16[2,2048,256]{2,1,0:T(8,128)(2,1)}, bf16[2,2048,256]{2,1,0:T(8,128)(2,1)}, u32[]{:S(2)}, u32[]{:S(2)}) collective-permute-start(bf16[2,2048,256]{2,1,0:T(8,128)(2,1)} %maximum_bitcast_fusion), channel_id=1, source_target_pairs={{0,4},{4,0},{8,12},{12,8},{1,5},{5,1},{9,13},{13,9},{2,6},{6,2},{1... | collective-permute-start | bytes 6291464 | tf_op jit(solution)/shard_map/ppermute | solution.py:16
  100.1 5.0 %copy-start.3 = (bf16[1,1,2048,256]{3,2,1,0:T(8,128)(2,1)S(1)}, bf16[1,1,2048,256]{3,2,1,0:T(8,128)(2,1)}, u32[]{:S(2)}) copy-start(bf16[1,1,2048,256]{3,2,1,0:T(8,128)(2,1)} %copy-done.2) | copy-start | bytes 3145732
  103.5 30.0 %collective-permute-start.9 = (bf16[4,512,256]{2,1,0:T(8,128)(2,1)}, bf16[4,512,256]{2,1,0:T(8,128)(2,1)}, u32[]{:S(2)}, u32[]{:S(2)}) collective-permute-start(bf16[4,512,256]{2,1,0:T(8,128)(2,1)} %bitcast.218), channel_id=1, source_target_pairs={{0,16},{16,0},{1,17},{17,1},{2,18},{18,2},{3,19},{19,3},{4,20},{20... | collective-permute-start | bytes 3145736 | tf_op jit(solution)/shard_map/ppermute | solution.py:16
  109.3 15.4 %copy-start.5 = (bf16[8,8,4,512]{3,1,2,0:T(8,128)(2,1)S(1)}, bf16[8,8,4,512]{3,1,2,0:T(8,128)(2,1)}, u32[]{:S(2)}) copy-start(bf16[8,8,4,512]{3,1,2,0:T(8,128)(2,1)} %copy.48) | copy-start | bytes 786436
  109.3 15.5 %copy-start.9 = (bf16[1,4,16,256]{3,2,1,0:T(8,128)(2,1)S(1)}, bf16[1,4,16,256]{3,2,1,0:T(8,128)(2,1)}, u32[]{:S(2)}) copy-start(bf16[1,4,16,256]{3,2,1,0:T(8,128)(2,1)} %copy.29) | copy-start | bytes 98308
  125.2 1.9 copy-start.4
  126.6 25.5 %collective-permute-start.6 = (bf16[4,512,256]{2,1,0:T(8,128)(2,1)}, bf16[4,512,256]{2,1,0:T(8,128)(2,1)S(1)}, u32[]{:S(2)}, u32[]{:S(2)}) collective-permute-start(bf16[4,512,256]{2,1,0:T(8,128)(2,1)} %bitcast.219), channel_id=1, source_target_pairs={{0,16},{16,0},{1,17},{17,1},{2,18},{18,2},{3,19},{19,3},{4,20},{20... | collective-permute-start | bytes 3145736 | tf_op jit(solution)/shard_map/ppermute | solution.py:16
  155.1 4.6 %copy-start.6 = (bf16[8,16,2048]{2,1,0:T(8,128)(2,1)S(1)}, bf16[8,16,2048]{2,1,0:T(8,128)(2,1)}, u32[]{:S(2)}) copy-start(bf16[8,16,2048]{2,1,0:T(8,128)(2,1)} %param.27) | copy-start | bytes 1572868
  155.1 4.6 %copy-start.11 = (s32[192]{0:T(256)S(1)}, s32[192]{0:T(256)}, u32[]{:S(2)}) copy-start(s32[192]{0:T(256)} %param.24) | copy-start | bytes 2308
  155.1 4.6 %copy-start.13 = (s32[128]{0:T(128)S(1)}, s32[128]{0:T(128)}, u32[]{:S(2)}) copy-start(s32[128]{0:T(128)} %and_select_fusion) | copy-start | bytes 1540
  155.1 30.3 %all-to-all-start = ((bf16[4,2,512,256]{3,2,1,0:T(8,128)(2,1)}), bf16[4,2,512,256]{3,2,1,0:T(8,128)(2,1)}, u32[]{:S(2)}, u32[]{:S(2)}) async-start(bf16[4,2,512,256]{3,2,1,0:T(8,128)(2,1)} %get-tuple-element.41), calls=%async_computation | async-start | bytes 4194304 | tf_op jit(solution)/shard_map/all_to_all | solution.py:167
  162.5 27.5 %collective-permute-start.12 = (f32[2,48,2048]{2,1,0:T(8,128)S(1)}, f32[2,48,2048]{2,1,0:T(8,128)S(1)}, u32[]{:S(2)}, u32[]{:S(2)}) collective-permute-start(f32[2,48,2048]{2,1,0:T(8,128)S(1)} %select_bitcast_fusion.8), channel_id=1, source_target_pairs={{0,1},{1,0},{2,3},{3,2},{4,5},{5,4},{6,7},{7,6},{8,9},{9,8},{10,11... | collective-permute-start | bytes 2359304 | tf_op jit(solution)/shard_map/ppermute | solution.py:16
  185.5 30.2 %all-to-all-start.1 = ((bf16[4,2,512,256]{3,2,1,0:T(8,128)(2,1)}), bf16[4,2,512,256]{3,2,1,0:T(8,128)(2,1)}, u32[]{:S(2)}, u32[]{:S(2)}) async-start(bf16[4,2,512,256]{3,2,1,0:T(8,128)(2,1)} %get-tuple-element.40), calls=%async_computation.1 | async-start | bytes 4194304 | tf_op jit(solution)/shard_map/all_to_all | solution.py:167
  190.1 20.9 %collective-permute-start.13 = (f32[1,48,2048]{2,1,0:T(8,128)S(1)}, f32[1,48,2048]{2,1,0:T(8,128)S(1)}, u32[]{:S(2)}, u32[]{:S(2)}) collective-permute-start(f32[1,48,2048]{2,1,0:T(8,128)S(1)} %select_bitcast_fusion.9), channel_id=1, source_target_pairs={{0,2},{1,3},{2,0},{3,1},{4,6},{5,7},{6,4},{7,5},{8,10},{9,11},{10,... | collective-permute-start | bytes 1179656 | tf_op jit(solution)/shard_map/ppermute | solution.py:16
  215.7 7.6 %copy-start.1 = (bf16[2048,256]{1,0:T(8,128)(2,1)S(1)}, bf16[2048,256]{1,0:T(8,128)(2,1)}, u32[]{:S(2)}) copy-start(bf16[2048,256]{1,0:T(8,128)(2,1)} %param.16) | copy-start | bytes 3145732

commit v2 on v1

--- a/solution.py
+++ b/solution.py
@@ -16,19 +16,23 @@
     return lax.ppermute(value, axis, pairs)
 
 
-def gathered(value, axis):
+def gathered(value, axis, after=None):
     size = lax.axis_size(axis)
     index = lax.axis_index(axis)
     held = value[None]
     mask = size // 2
+    arrived = None
     while mask >= 1:
         other = exchanged(held, axis, mask)
+        if after is not None:
+            other = lax.optimization_barrier((other, after))[0]
+        arrived = other if arrived is None else arrived
         low_bit = (index // mask) % 2 == 0
         first = jnp.where(low_bit, held, other)
         second = jnp.where(low_bit, other, held)
         held = jnp.stack([first, second], axis=1).reshape((-1,) + value.shape)
         mask //= 2
-    return held
+    return held, arrived
 
 
 def scattered_sum(value, axis):
@@ -53,33 +57,40 @@
     start = pl.program_id(0) * rows
     lane = lax.broadcasted_iota(jnp.int32, (groups, 2 * positions), 1)
     factor = HEAD_DIM ** (-0.5)
+    blocks, scores, owns = [], [], []
     for row in range(rows):
         pairs = cache_ref[row].reshape(2 * positions, kv_heads * HEAD_DIM)
-        length = lengths[start + row]
-        valid = (lane % 2 == 0) & (lane < 2 * length)
+        valid = (lane % 2 == 0) & (lane < 2 * lengths[start + row])
         for head in range(kv_heads):
             block = pairs[:, head * HEAD_DIM : (head + 1) * HEAD_DIM]
             query = query_ref[row, head * groups : (head + 1) * groups, :]
             own_key = key_ref[row, head : head + 1, :].astype(jnp.float32)
+            own = jnp.sum(query.astype(jnp.float32) * own_key, axis=1, keepdims=True) * factor
+            score = lax.dot_general(
+                query, block, (((1,), (1,)), ((), ())), preferred_element_type=jnp.float32
+            )
+            blocks.append(block)
+            scores.append(jnp.where(valid, score * factor, -1e30))
+            owns.append(own)
+    scores = jnp.concatenate(scores, axis=0)
+    own = jnp.concatenate(owns, axis=0)
+    highest = jnp.maximum(jnp.max(scores, axis=1, keepdims=True), own)
+    raw = jnp.where(scores > -1e29, jnp.exp(scores - highest), 0.0)
+    own_raw = jnp.exp(own - highest)
+    total = jnp.sum(raw, axis=1, keepdims=True) + own_raw
+    weights = pltpu.roll(raw / total, 1, 1).astype(jnp.bfloat16)
+    own_weight = (own_raw / total).astype(jnp.bfloat16).astype(jnp.float32)
+    for row in range(rows):
+        for head in range(kv_heads):
+            at = (row * kv_heads + head) * groups
             own_value = value_ref[row, head : head + 1, :].astype(jnp.float32)
-            scores = (
-                lax.dot_general(
-                    query, block, (((1,), (1,)), ((), ())), preferred_element_type=jnp.float32
-                )
-                * factor
+            mixed = jnp.dot(
+                weights[at : at + groups],
+                blocks[row * kv_heads + head],
+                preferred_element_type=jnp.float32,
             )
-            own = jnp.sum(query.astype(jnp.float32) * own_key, axis=1, keepdims=True) * factor
-            highest = jnp.maximum(
-                jnp.max(jnp.where(valid, scores, -1e30), axis=1, keepdims=True), own
-            )
-            raw = jnp.where(valid, jnp.exp(scores - highest), 0.0)
-            own_raw = jnp.exp(own - highest)
-            total = jnp.sum(raw, axis=1, keepdims=True) + own_raw
-            weights = pltpu.roll(raw / total, 1, 1).astype(jnp.bfloat16)
-            own_weight = (own_raw / total).astype(jnp.bfloat16).astype(jnp.float32)
-            mixed = jnp.dot(weights, block, preferred_element_type=jnp.float32)
             out_ref[row, head * groups : (head + 1) * groups, :] = (
-                mixed + own_weight * own_value
+                mixed + own_weight[at : at + groups] * own_value
             ).astype(jnp.bfloat16)
 
 
@@ -157,14 +168,16 @@
     return owner_hit[:, None, :] & slot_hit[None, :, :]
 
 
-def hand_over(block, hits):
-    arrived = exchanged(block, "pool", 1)
-    outgoing = jnp.zeros(hits.shape[:2] + block.shape[1:], block.dtype)
-    for request in range(block.shape[0]):
+def hand_over(arrived, hits, after):
+    if after is not None:
+        arrived = lax.optimization_barrier((arrived, after))[0]
+    outgoing = jnp.zeros(hits.shape[:2] + arrived.shape[1:], arrived.dtype)
+    for request in range(arrived.shape[0]):
         outgoing = jnp.where(
             hits[:, :, request][:, :, None, None], arrived[request][None, None], outgoing
         )
-    return lax.all_to_all(outgoing, "seq", split_axis=0, concat_axis=0, tiled=True)
+    landed = lax.all_to_all(outgoing, "seq", split_axis=0, concat_axis=0, tiled=True)
+    return landed, outgoing
 
 
 def body(
@@ -201,12 +214,16 @@
         pick, adapter_down_weight, (((1,), (1,)), ((), ())), preferred_element_type=jnp.float32
     ).astype(jnp.bfloat16)
     matrix = key_value_weight.reshape(shard, 2 * width)
-    down_all = gathered(down, "seq")
-    key_all = gathered(matrix[:, :width], "seq").reshape(model_width, width)
-    value_all = gathered(matrix[:, width:], "seq").reshape(model_width, width)
+    down_all, down_first = gathered(down, "seq")
+    matrix = lax.optimization_barrier((matrix, down_first))[0]
+    key_all, key_first = gathered(matrix[:, :width], "seq")
+    value_all, _ = gathered(matrix[:, width:], "seq", key_all)
+    key_all = key_all.reshape(model_width, width)
+    value_all = value_all.reshape(model_width, width)
+    rotated_query = lax.optimization_barrier((rotated_query, key_first))[0]
 
     attended = attend(rotated_query, key_value_cache, current_key_value, cached_length)
-    attn_rows = gathered(attended, "seq").reshape(-1, attended.shape[1])
+    attn_rows = gathered(attended, "seq")[0].reshape(-1, attended.shape[1])
     ranks = ADAPTER_COUNT * ADAPTER_RANK
     down_flat = output_down_weight.reshape(output_down_weight.shape[0], ranks)
     up_flat = output_up_weight.reshape(ranks, output_up_weight.shape[2])
@@ -222,7 +239,7 @@
     my_tokens = lax.dynamic_slice_in_dim(prompt, mine, share, axis=0)
     my_down = down_all.transpose(1, 0, 2).reshape(share, columns, model_width)
     my_low = jnp.einsum("rtk,rck->rct", my_tokens, my_down, preferred_element_type=jnp.float32)
-    low = gathered(my_low, "head") if share < requests else my_low[None]
+    low = gathered(my_low, "head")[0] if share < requests else my_low[None]
     low = low.reshape(requests, 2, ADAPTER_RANK, tok_dev).astype(jnp.bfloat16)
     own = jnp.eye(requests, dtype=jnp.bool_)[None, :, None, :, None]
     spread = jnp.where(
@@ -241,14 +258,18 @@
     other_owners = lax.dynamic_slice_in_dim(destination, (1 - pool_index) * requests, requests)
     hits = slot_hits(other_owners, decoders)
 
-    handed = []
+    arrived = []
     for which, weight in enumerate((key_all, value_all)):
         base = jnp.dot(tokens, weight, preferred_element_type=jnp.float32)
         extra = lax.dot_general(
             spread[which], up[which], (((0,), (0,)), ((), ())), preferred_element_type=jnp.float32
         )
         block = (base + extra).astype(jnp.bfloat16).reshape(requests, tok_dev, width)
-        handed.append(hand_over(block, hits))
+        arrived.append(exchanged(block, "pool", 1))
+    handed, outgoing = [], block
+    for blocks in arrived:
+        landed, outgoing = hand_over(blocks, hits, outgoing)
+        handed.append(landed)
     return (weave(handed[0], handed[1]), decoded)
 
 

time: 224 us -> 194 us (0.87)
  Pallas kernels: 48.5 us -> 16.9 us
  other arithmetic: 14.7 us -> 17.7 us
  matrix products: 50.6 us -> 48.2 us
    pallas_call x1, Pallas kernels: 40.9 us -> 9.27 us  [attend(): pl.pallas_call(attend_kernel, grid_spec=pltpu.PrefetchScalarGridSpec(num_...]
    all_to_all x2, waiting for transfers between devices: 25.3 us -> 8.39 us  [hand_over(): lax.all_to_all(outgoing, 'seq', split_axis=0, concat_axis=0, tiled=True)]
    ppermute x14, waiting for transfers between devices: 42 us -> 57.2 us  [exchanged(): return lax.ppermute(value, axis, pairs)]
    dot_general x1, matrix products: 6.36 us -> 3.06 us  [body(): jnp.dot(attn_rows, output_weight, preferred_element_type=jnp.float32)]
    another operation x14 -> x15, other arithmetic: 7.78 us -> 8.11 us  [gathered(): held = jnp.stack([first, second], axis=1).reshape((-1,) + value.shape)]
  transfers between devices with their start and end apart: 16 -> 16, of which waited for: 7 -> 10; matrix products, arithmetic and copies ran while one was open for 33% -> 40% of each run, Pallas kernels for 18% -> 5%
where the time goes in v2:
time: 194 us; the launch traced here: 193 us
  waiting for transfers between devices  65.5 us (34%)
  matrix products  48.2 us (25%)
  starting transfers between devices  26.8 us (14%)
  other arithmetic  17.7 us (9%)
  Pallas kernels  16.9 us (9%)
  local copies, waits for them, and re-layouts  16.5 us (9%)
    ppermute x14, waiting for transfers between devices, exchanged(): return lax.ppermute(value, axis, pairs)  57.2 us
    dot_general x2, matrix products, body(): base = jnp.dot(tokens, weight, preferred_element_type=jnp.float32)  32.4 us
    ppermute x14, starting transfers between devices, exchanged(): return lax.ppermute(value, axis, pairs)  17.8 us
    pallas_call x1, Pallas kernels, attend(): pl.pallas_call(attend_kernel, grid_spec=pltpu.PrefetchScalarGridSpec(num_...  9.27 us
    all_to_all x2, starting transfers between devices, hand_over(): lax.all_to_all(outgoing, 'seq', split_axis=0, concat_axis=0, tiled=True)  9.03 us
    all_to_all x2, waiting for transfers between devices, hand_over(): lax.all_to_all(outgoing, 'seq', split_axis=0, concat_axis=0, tiled=True)  8.39 us
    another operation x15, other arithmetic, gathered(): held = jnp.stack([first, second], axis=1).reshape((-1,) + value.shape)  8.11 us
    pallas_call x1, Pallas kernels, weave(): pl.pallas_call(weave_kernel, grid=(slots, sources), in_specs=[spec, spec]...  7.61 us
  transfers between devices with their start and end apart: 16, of which 10 were waited for; matrix products, arithmetic and copies ran while one was open for 40% of the time, Pallas kernels for 5%

profile of v2, /device:TPU:0, one launch (start us, length us, event | category | flops | bytes accessed | tf_op | source)
XLA Modules:
  0.0 193.5 jit_solution(15698170936103945559)
XLA Ops:
  3.0 3.0 %collective-permute-start = (bf16[1,32,2048]{2,1,0:T(8,128)(2,1)S(1)}, bf16[1,32,2048]{2,1,0:T(8,128)(2,1)S(1)}, u32[]{:S(2)}, u32[]{:S(2)}) collective-permute-start(bf16[1,32,2048]{2,1,0:T(8,128)(2,1)S(1)} %fusion.5), channel_id=1, source_target_pairs={{0,8},{4,12},{8,0},{12,4},{1,9},{5,13},{9,1},{13,5},{2,10},{6,14},... | collective-permute-start | bytes 393224 | tf_op jit(solution)/shard_map/ppermute | solution.py:16
  8.3 2.0 %copy.46 = bf16[256,8,2,256]{3,1,2,0:T(8,128)(2,1)S(1)} copy(bf16[256,8,2,256]{3,2,1,0:T(2,128)(2,1)} %bitcast.219) | data formatting | bytes 4194304
  13.1 6.0 %fusion.8 = bf16[1,1,32,512]{3,2,1,0:T(8,128)(2,1)S(1)} fusion(bf16[32,8192]{1,0:T(8,128)(2,1)S(1)} %bitcast.216, bf16[4,512,8192]{2,1,0:T(8,128)(2,1)} %param.14, s32[]{:T(128)S(6)} %select_n.271), kind=kOutput, calls=%fused_computation.26 | convolution fusion | flops 268435456 | bytes 8945668 | tf_op jit(solution)/shard_map/rtk,rck->rct/dot_general | solution.py:241
  19.1 2.6 %collective-permute-start.4 = (bf16[1,1,32,512]{3,2,1,0:T(8,128)(2,1)S(1)}, bf16[1,1,32,512]{3,2,1,0:T(8,128)(2,1)S(1)}, u32[]{:S(2)}, u32[]{:S(2)}) collective-permute-start(bf16[1,1,32,512]{3,2,1,0:T(8,128)(2,1)S(1)} %fusion.8), channel_id=1, source_target_pairs={{0,2},{1,3},{2,0},{3,1},{4,6},{5,7},{6,4},{7,5},{8,10},{9,11},{10,... | collective-permute-start | bytes 98312 | tf_op jit(solution)/shard_map/ppermute | solution.py:16
  24.0 1.6 collective-permute-start.5
  28.4 10.1 %collective-permute-done.1 = bf16[1,2048,256]{2,1,0:T(8,128)(2,1)} collective-permute-done((bf16[1,2048,256]{2,1,0:T(8,128)(2,1)}, bf16[1,2048,256]{2,1,0:T(8,128)(2,1)}, u32[]{:S(2)}, u32[]{:S(2)}) %collective-permute-start.1) | collective-permute-done | bytes 1048608 | tf_op jit(solution)/shard_map/ppermute | solution.py:16
  39.3 9.3 %shard_map.150 = bf16[48,16,128]{2,1,0:T(8,128)(2,1)} custom-call(s32[48]{0:T(128)} %lengths.1, bf16[48,16,128]{2,1,0:T(8,128)(2,1)} %bitcast.226, bf16[48,128,2,256]{3,2,1,0:T(2,128)(2,1)} %cache_ref.1, bf16[48,2,128]{2,1,0:T(2,128)(2,1)} %reshape_squeeze.6.key_ref, bf16[48,2,128]{2,1,0:T(2,128)(2,1)} %reshape_squeeze.7.value_ref), custom_call_target="tpu_custom_call" | custom-call | flops 100663296 | bytes 6291456 | tf_op jit(solution)/shard_map/pallas_call | solution.py:105
  50.3 1.5 select_bitcast_fusion.7
  52.1 12.5 %collective-permute-done.10 = bf16[1,48,2048]{2,1,0:T(8,128)(2,1)S(1)} collective-permute-done((bf16[1,48,2048]{2,1,0:T(8,128)(2,1)S(1)}, bf16[1,48,2048]{2,1,0:T(8,128)(2,1)S(1)}, u32[]{:S(2)}, u32[]{:S(2)}) %collective-permute-start.10) | collective-permute-done | bytes 196640 | tf_op jit(solution)/shard_map/ppermute | solution.py:16
  66.7 3.1 %fusion.30 = f32[192,2048]{1,0:T(8,128)} fusion(bf16[192,2048]{1,0:T(8,128)(2,1)S(1)} %bitcast.214, bf16[2048,2048]{1,0:T(8,128)(2,1)S(1)} %bitcast.234), kind=kOutput, calls=%fused_computation.103 | convolution fusion | flops 1610612736 | bytes 10747904 | tf_op jit(solution)/shard_map/dot_general | solution.py:233
  70.1 2.4 %pad_maximum_fusion = bf16[2,2,2048,256]{3,2,1,0:T(8,128)(2,1)} fusion(bf16[2,1,2048,256]{3,2,1,0:T(8,128)(2,1)S(1)} %get-tuple-element.19, bf16[2,1,2048,256]{3,2,1,0:T(8,128)(2,1)S(1)} %get-tuple-element.18), kind=kLoop, calls=%fused_computation.3 | loop fusion | flops 2097152 | bytes 8388608 | tf_op jit(solution)/shard_map/stack | solution.py:33
  73.8 1.8 maximum_bitcast_fusion.1
  75.7 17.0 %convolution_bitcast_fusion.1 = f32[2048,256]{0,1:T(8,128)} fusion(bf16[8192,256]{1,0:T(8,128)(2,1)} %bitcast.212, bf16[2048,8192]{1,0:T(8,128)(2,1)} %bitcast.217), kind=kOutput, calls=%fused_computation.8 | convolution fusion | flops 8589934592 | bytes 39845888 | tf_op jit(solution)/shard_map/dot_general | solution.py:263
  92.7 2.2 %fusion.3 = bf16[2048,256]{0,1:T(8,128)(2,1)S(1)} fusion(f32[2048,256]{0,1:T(8,128)} %convolution_bitcast_fusion.1, bf16[64,2048]{1,0:T(8,128)(2,1)S(1)} %bitcast.225, bf16[64,256]{1,0:T(8,128)(2,1)S(1)} %bitcast.232), kind=kOutput, calls=%fused_computation.9 | convolution fusion | flops 68157440 | bytes 3440640 | tf_op jit(solution)/shard_map/dot_general | solution.py:264
  96.2 1.5 collective-permute-start.6
  97.7 1.9 select_bitcast_fusion.1
  100.0 2.3 %copy.32 = bf16[2,2,2048,256]{3,2,1,0:T(8,128)(2,1)} copy(bf16[2,2,2048,256]{3,2,0,1:T(8,128)(2,1)S(1)} %pad_maximum_fusion.1) | data formatting | bytes 8388608 | tf_op jit(solution)/shard_map/stack | solution.py:33
  102.3 15.4 %convolution_bitcast_fusion = f32[2048,256]{0,1:T(8,128)S(1)} fusion(bf16[8192,256]{1,0:T(8,128)(2,1)} %bitcast.213, bf16[2048,8192]{1,0:T(8,128)(2,1)} %bitcast.218), kind=kOutput, calls=%fused_computation.6 | convolution fusion | flops 8589934592 | bytes 39845888 | tf_op jit(solution)/shard_map/dot_general | solution.py:263
  118.9 1.6 copy.35
  121.9 1.6 collective-permute-start.9
  123.5 1.8 select_select_fusion.1
  125.3 4.6 %all-to-all-start = ((bf16[4,2,512,256]{3,2,1,0:T(8,128)(2,1)}), bf16[4,2,512,256]{3,2,1,0:T(8,128)(2,1)}, u32[]{:S(2)}, u32[]{:S(2)}) async-start(bf16[4,2,512,256]{3,2,1,0:T(8,128)(2,1)} %select_select_fusion.1), calls=%async_computation | async-start | bytes 4194304 | tf_op jit(solution)/shard_map/all_to_all | solution.py:179
  130.0 2.6 %convolution_add_fusion.2 = f32[192,2048]{1,0:T(8,128)S(1)} fusion(f32[192,2048]{1,0:T(8,128)} %fusion.30, bf16[128,2048]{1,0:T(8,128)(2,1)S(1)} %bitcast.227, bf16[192,2048]{1,0:T(8,128)(2,1)S(1)} %bitcast.215, bf16[2048,128]{0,1:T(8,128)(2,1)} %bitcast.228, s32[128]{0:T(128)S(1)} %copy-done.10, s32[192]{0:T(256)S(1)} %copy-done.9), kind=kOutput, calls=%fused_computation.11 | convolution fusion | flops 201793536 | bytes 4982016 | tf_op jit(solution)/shard_map/dot_general | solution.py:234
  132.7 1.6 collective-permute-start.12
  134.3 12.6 %collective-permute-done.9 = bf16[4,512,256]{2,1,0:T(8,128)(2,1)} collective-permute-done((bf16[4,512,256]{2,1,0:T(8,128)(2,1)}, bf16[4,512,256]{2,1,0:T(8,128)(2,1)}, u32[]{:S(2)}, u32[]{:S(2)}) %collective-permute-start.9) | collective-permute-done | bytes 1048608 | tf_op jit(solution)/shard_map/ppermute | solution.py:16
  148.2 1.9 select_select_fusion
  150.1 5.6 %all-to-all-done.key_ref = bf16[4,2,512,256]{3,2,1,0:T(8,128)(2,1)} async-done(((bf16[4,2,512,256]{3,2,1,0:T(8,128)(2,1)}), bf16[4,2,512,256]{3,2,1,0:T(8,128)(2,1)}, u32[]{:S(2)}, u32[]{:S(2)}) %all-to-all-start) | async-done | bytes 2097184 | tf_op jit(solution)/shard_map/all_to_all | solution.py:179
  155.7 4.5 %all-to-all-start.1 = ((bf16[4,2,512,256]{3,2,1,0:T(8,128)(2,1)}), bf16[4,2,512,256]{3,2,1,0:T(8,128)(2,1)}, u32[]{:S(2)}, u32[]{:S(2)}) async-start(bf16[4,2,512,256]{3,2,1,0:T(8,128)(2,1)} %select_select_fusion), calls=%async_computation.1 | async-start | bytes 4194304 | tf_op jit(solution)/shard_map/all_to_all | solution.py:179
  161.4 2.6 %collective-permute-start.13 = (f32[1,48,2048]{2,1,0:T(8,128)S(1)}, f32[1,48,2048]{2,1,0:T(8,128)S(1)}, u32[]{:S(2)}, u32[]{:S(2)}) collective-permute-start(f32[1,48,2048]{2,1,0:T(8,128)S(1)} %select_bitcast_fusion.9), channel_id=1, source_target_pairs={{0,2},{1,3},{2,0},{3,1},{4,6},{5,7},{6,4},{7,5},{8,10},{9,11},{10,... | collective-permute-start | bytes 1179656 | tf_op jit(solution)/shard_map/ppermute | solution.py:16
  164.1 18.2 %collective-permute-done.13 = f32[1,48,2048]{2,1,0:T(8,128)S(1)} collective-permute-done((f32[1,48,2048]{2,1,0:T(8,128)S(1)}, f32[1,48,2048]{2,1,0:T(8,128)S(1)}, u32[]{:S(2)}, u32[]{:S(2)}) %collective-permute-start.13) | collective-permute-done | bytes 393248 | tf_op jit(solution)/shard_map/ppermute | solution.py:16
  183.1 2.8 %all-to-all-done.1.value_ref = bf16[4,2,512,256]{3,2,1,0:T(8,128)(2,1)} async-done(((bf16[4,2,512,256]{3,2,1,0:T(8,128)(2,1)}), bf16[4,2,512,256]{3,2,1,0:T(8,128)(2,1)}, u32[]{:S(2)}, u32[]{:S(2)}) %all-to-all-start.1) | async-done | bytes 2097184 | tf_op jit(solution)/shard_map/all_to_all | solution.py:179
  185.8 7.6 %shard_map.149 = bf16[1,2,2048,2,256]{4,3,2,1,0:T(2,128)(2,1)} custom-call(bf16[4,2,512,256]{3,2,1,0:T(8,128)(2,1)} %all-to-all-done.key_ref, bf16[4,2,512,256]{3,2,1,0:T(8,128)(2,1)} %all-to-all-done.1.value_ref), custom_call_target="tpu_custom_call" | custom-call | flops 1073741824 | bytes 8388608 | tf_op jit(solution)/shard_map/pallas_call | solution.py:145
  (99 shorter events, 26.0 us)
Async XLA Ops:
  0.6 2.0 %copy-start = (bf16[2048,256]{1,0:T(8,128)(2,1)S(1)}, bf16[2048,256]{1,0:T(8,128)(2,1)}, u32[]{:S(2)}) copy-start(bf16[2048,256]{1,0:T(8,128)(2,1)} %param.16) | copy-start | bytes 3145732
  3.0 7.5 %collective-permute-start = (bf16[1,32,2048]{2,1,0:T(8,128)(2,1)S(1)}, bf16[1,32,2048]{2,1,0:T(8,128)(2,1)S(1)}, u32[]{:S(2)}, u32[]{:S(2)}) collective-permute-start(bf16[1,32,2048]{2,1,0:T(8,128)(2,1)S(1)} %fusion.5), channel_id=1, source_target_pairs={{0,8},{4,12},{8,0},{12,4},{1,9},{5,13},{9,1},{13,5},{2,10},{6,14},... | collective-permute-start | bytes 393224 | tf_op jit(solution)/shard_map/ppermute | solution.py:16
  8.3 2.1 %copy-start.8 = (bf16[48,2,256]{2,1,0:T(2,128)(2,1)S(1)}, bf16[48,2,256]{2,1,0:T(2,128)(2,1)}, u32[]{:S(2)}) copy-start(bf16[48,2,256]{2,1,0:T(2,128)(2,1)} %param.22) | copy-start | bytes 147460
  10.7 2.2 %collective-permute-start.3 = (bf16[2,32,2048]{2,1,0:T(8,128)(2,1)S(1)}, bf16[2,32,2048]{2,1,0:T(8,128)(2,1)S(1)}, u32[]{:S(2)}, u32[]{:S(2)}) collective-permute-start(bf16[2,32,2048]{2,1,0:T(8,128)(2,1)S(1)} %maximum_bitcast_fusion.3), channel_id=1, source_target_pairs={{0,4},{4,0},{8,12},{12,8},{1,5},{5,1},{9,13},{13,9},{2,6},{6,2},{1... | collective-permute-start | bytes 786440 | tf_op jit(solution)/shard_map/ppermute | solution.py:16
  12.2 26.3 %collective-permute-start.1 = (bf16[1,2048,256]{2,1,0:T(8,128)(2,1)}, bf16[1,2048,256]{2,1,0:T(8,128)(2,1)}, u32[]{:S(2)}, u32[]{:S(2)}) collective-permute-start(bf16[1,2048,256]{2,1,0:T(8,128)(2,1)} %get-tuple-element.25), channel_id=1, source_target_pairs={{0,8},{4,12},{8,0},{12,4},{1,9},{5,13},{9,1},{13,5},{2,10},{6,14},... | collective-permute-start | bytes 3145736 | tf_op jit(solution)/shard_map/ppermute | solution.py:16
  13.1 25.4 %copy-start.7 = (bf16[48,2048]{1,0:T(8,128)(2,1)S(1)}, bf16[48,2048]{1,0:T(8,128)(2,1)}, u32[]{:S(2)}) copy-start(bf16[48,2048]{1,0:T(8,128)(2,1)} %param.20) | copy-start | bytes 589828
  19.1 4.8 %collective-permute-start.4 = (bf16[1,1,32,512]{3,2,1,0:T(8,128)(2,1)S(1)}, bf16[1,1,32,512]{3,2,1,0:T(8,128)(2,1)S(1)}, u32[]{:S(2)}, u32[]{:S(2)}) collective-permute-start(bf16[1,1,32,512]{3,2,1,0:T(8,128)(2,1)S(1)} %fusion.8), channel_id=1, source_target_pairs={{0,2},{1,3},{2,0},{3,1},{4,6},{5,7},{6,4},{7,5},{8,10},{9,11},{10,... | collective-permute-start | bytes 98312 | tf_op jit(solution)/shard_map/ppermute | solution.py:16
  24.0 4.3 %collective-permute-start.5 = (bf16[2,1,32,512]{3,2,0,1:T(8,128)(2,1)S(1)}, bf16[2,1,32,512]{3,2,0,1:T(8,128)(2,1)S(1)}, u32[]{:S(2)}, u32[]{:S(2)}) collective-permute-start(bf16[2,1,32,512]{3,2,0,1:T(8,128)(2,1)S(1)} %maximum_bitcast_fusion.4), channel_id=1, source_target_pairs={{0,1},{1,0},{2,3},{3,2},{4,5},{5,4},{6,7},{7,6},{8,9},{9,8},{10,11... | collective-permute-start | bytes 196616 | tf_op jit(solution)/shard_map/ppermute | solution.py:16
  26.2 46.2 %collective-permute-start.7 = (bf16[1,2048,256]{2,1,0:T(8,128)(2,1)}, bf16[1,2048,256]{2,1,0:T(8,128)(2,1)}, u32[]{:S(2)}, u32[]{:S(2)}) collective-permute-start(bf16[1,2048,256]{2,1,0:T(8,128)(2,1)} %get-tuple-element.24), channel_id=1, source_target_pairs={{0,8},{4,12},{8,0},{12,4},{1,9},{5,13},{9,1},{13,5},{2,10},{6,14},... | collective-permute-start | bytes 3145736 | tf_op jit(solution)/shard_map/ppermute | solution.py:16
  49.5 15.1 %collective-permute-start.10 = (bf16[1,48,2048]{2,1,0:T(8,128)(2,1)S(1)}, bf16[1,48,2048]{2,1,0:T(8,128)(2,1)S(1)}, u32[]{:S(2)}, u32[]{:S(2)}) collective-permute-start(bf16[1,48,2048]{2,1,0:T(8,128)(2,1)S(1)} %broadcast_in_dim_reshape.4), channel_id=1, source_target_pairs={{0,8},{4,12},{8,0},{12,4},{1,9},{5,13},{9,1},{13,5},{2,10},{6,14},... | collective-permute-start | bytes 589832 | tf_op jit(solution)/shard_map/ppermute | solution.py:16
  50.3 16.4 %slice-start = ((s8[8388608]{0:T(1024)(128)(4,1)}), s8[4194304]{0:T(1024)(128)(4,1)S(1)}, s32[]{:S(2)}) async-start(s8[8388608]{0:T(1024)(128)(4,1)} %bitcast.233), calls=%async_computation.2 | async-start | bytes 8388608
  51.8 13.0 %copy-start.11 = (pred[4,4]{1,0:T(4,128)(4,1)S(1)}, pred[4,4]{1,0:T(4,128)(4,1)}, u32[]{:S(2)}) copy-start(pred[4,4]{1,0:T(4,128)(4,1)} %iota_compare_fusion.3) | copy-start | bytes 52
  51.8 14.9 %slice-start.1 = ((s8[8388608]{0:T(1024)(128)(4,1)}), s8[4194304]{0:T(1024)(128)(4,1)S(1)}, s32[]{:S(2)}) async-start(s8[8388608]{0:T(1024)(128)(4,1)} %bitcast.233), calls=%async_computation.3 | async-start | bytes 8388608
  52.0 17.7 %collective-permute-start.2 = (bf16[2,2048,256]{2,1,0:T(8,128)(2,1)S(1)}, bf16[2,2048,256]{2,1,0:T(8,128)(2,1)S(1)}, u32[]{:S(2)}, u32[]{:S(2)}) collective-permute-start(bf16[2,2048,256]{2,1,0:T(8,128)(2,1)S(1)} %maximum_bitcast_fusion), channel_id=1, source_target_pairs={{0,4},{4,0},{8,12},{12,8},{1,5},{5,1},{9,13},{13,9},{2,6},{6,2},{1... | collective-permute-start | bytes 6291464 | tf_op jit(solution)/shard_map/ppermute | solution.py:16
  64.7 1.8 collective-permute-start.11
  66.7 3.1 %copy-start.4 = (bf16[2,2,48,2048]{3,2,1,0:T(8,128)(2,1)}, bf16[2,2,48,2048]{3,2,1,0:T(8,128)(2,1)S(1)}, u32[]{:S(2)}) copy-start(bf16[2,2,48,2048]{3,2,1,0:T(8,128)(2,1)S(1)} %pad_maximum_fusion.2) | copy-start | bytes 2359300
  73.8 1.8 copy-start.2
  75.6 22.1 %collective-permute-start.8 = (bf16[2,2048,256]{2,1,0:T(8,128)(2,1)}, bf16[2,2048,256]{2,1,0:T(8,128)(2,1)}, u32[]{:S(2)}, u32[]{:S(2)}) collective-permute-start(bf16[2,2048,256]{2,1,0:T(8,128)(2,1)} %maximum_bitcast_fusion.1), channel_id=1, source_target_pairs={{0,4},{4,0},{8,12},{12,8},{1,5},{5,1},{9,13},{13,9},{2,6},{6,2},{1... | collective-permute-start | bytes 6291464 | tf_op jit(solution)/shard_map/ppermute | solution.py:16
  92.7 5.0 %copy-start.3 = (bf16[1,1,2048,256]{3,2,1,0:T(8,128)(2,1)S(1)}, bf16[1,1,2048,256]{3,2,1,0:T(8,128)(2,1)}, u32[]{:S(2)}) copy-start(bf16[1,1,2048,256]{3,2,1,0:T(8,128)(2,1)} %copy-done.2) | copy-start | bytes 3145732
  96.2 25.6 %collective-permute-start.6 = (bf16[4,512,256]{2,1,0:T(8,128)(2,1)}, bf16[4,512,256]{2,1,0:T(8,128)(2,1)S(1)}, u32[]{:S(2)}, u32[]{:S(2)}) collective-permute-start(bf16[4,512,256]{2,1,0:T(8,128)(2,1)} %bitcast.221), channel_id=1, source_target_pairs={{0,16},{16,0},{1,17},{17,1},{2,18},{18,2},{3,19},{19,3},{4,20},{20... | collective-permute-start | bytes 3145736 | tf_op jit(solution)/shard_map/ppermute | solution.py:16
  121.9 25.0 %collective-permute-start.9 = (bf16[4,512,256]{2,1,0:T(8,128)(2,1)}, bf16[4,512,256]{2,1,0:T(8,128)(2,1)}, u32[]{:S(2)}, u32[]{:S(2)}) collective-permute-start(bf16[4,512,256]{2,1,0:T(8,128)(2,1)} %copy.35), channel_id=1, source_target_pairs={{0,16},{16,0},{1,17},{17,1},{2,18},{18,2},{3,19},{19,3},{4,20},{20... | collective-permute-start | bytes 3145736 | tf_op jit(solution)/shard_map/ppermute | solution.py:16
  125.3 4.6 %copy-start.5 = (bf16[2,2,48,2048]{3,2,1,0:T(8,128)(2,1)S(1)}, bf16[2,2,48,2048]{3,2,1,0:T(8,128)(2,1)}, u32[]{:S(2)}) copy-start(bf16[2,2,48,2048]{3,2,1,0:T(8,128)(2,1)} %copy-done.4) | copy-start | bytes 2359300
  125.3 4.6 %copy-start.6 = (bf16[8,16,2048]{2,1,0:T(8,128)(2,1)S(1)}, bf16[8,16,2048]{2,1,0:T(8,128)(2,1)}, u32[]{:S(2)}) copy-start(bf16[8,16,2048]{2,1,0:T(8,128)(2,1)} %param.27) | copy-start | bytes 1572868
  125.3 4.6 %copy-start.9 = (s32[192]{0:T(256)S(1)}, s32[192]{0:T(256)}, u32[]{:S(2)}) copy-start(s32[192]{0:T(256)} %param.24) | copy-start | bytes 2308
  125.3 4.6 %copy-start.10 = (s32[128]{0:T(128)S(1)}, s32[128]{0:T(128)}, u32[]{:S(2)}) copy-start(s32[128]{0:T(128)} %and_select_fusion) | copy-start | bytes 1540
  125.3 30.3 %all-to-all-start = ((bf16[4,2,512,256]{3,2,1,0:T(8,128)(2,1)}), bf16[4,2,512,256]{3,2,1,0:T(8,128)(2,1)}, u32[]{:S(2)}, u32[]{:S(2)}) async-start(bf16[4,2,512,256]{3,2,1,0:T(8,128)(2,1)} %select_select_fusion.1), calls=%async_computation | async-start | bytes 4194304 | tf_op jit(solution)/shard_map/all_to_all | solution.py:179
  132.7 27.4 %collective-permute-start.12 = (f32[2,48,2048]{2,1,0:T(8,128)S(1)}, f32[2,48,2048]{2,1,0:T(8,128)}, u32[]{:S(2)}, u32[]{:S(2)}) collective-permute-start(f32[2,48,2048]{2,1,0:T(8,128)S(1)} %select_bitcast_fusion.8), channel_id=1, source_target_pairs={{0,1},{1,0},{2,3},{3,2},{4,5},{5,4},{6,7},{7,6},{8,9},{9,8},{10,11... | collective-permute-start | bytes 2359304 | tf_op jit(solution)/shard_map/ppermute | solution.py:16
  155.7 30.2 %all-to-all-start.1 = ((bf16[4,2,512,256]{3,2,1,0:T(8,128)(2,1)}), bf16[4,2,512,256]{3,2,1,0:T(8,128)(2,1)}, u32[]{:S(2)}, u32[]{:S(2)}) async-start(bf16[4,2,512,256]{3,2,1,0:T(8,128)(2,1)} %select_select_fusion), calls=%async_computation.1 | async-start | bytes 4194304 | tf_op jit(solution)/shard_map/all_to_all | solution.py:179
  161.4 20.9 %collective-permute-start.13 = (f32[1,48,2048]{2,1,0:T(8,128)S(1)}, f32[1,48,2048]{2,1,0:T(8,128)S(1)}, u32[]{:S(2)}, u32[]{:S(2)}) collective-permute-start(f32[1,48,2048]{2,1,0:T(8,128)S(1)} %select_bitcast_fusion.9), channel_id=1, source_target_pairs={{0,2},{1,3},{2,0},{3,1},{4,6},{5,7},{6,4},{7,5},{8,10},{9,11},{10,... | collective-permute-start | bytes 1179656 | tf_op jit(solution)/shard_map/ppermute | solution.py:16
  185.8 7.6 %copy-start.1 = (bf16[2048,256]{1,0:T(8,128)(2,1)S(1)}, bf16[2048,256]{1,0:T(8,128)(2,1)}, u32[]{:S(2)}) copy-start(bf16[2048,256]{1,0:T(8,128)(2,1)} %param.16) | copy-start | bytes 3145732
